TPU v7x, 256 devices: a whole 4x4x8 slice. The times are simulated.
256 devices in a mesh: grp: 4 (over y_hi, core), blk: 64 (over z, x, y_lo).
Axes of the slice: x: 4, y: 4 (y_hi: 2, y_lo: 2; y = y_hi * 2 + y_lo), z: 8, core: 2. Of those that a mesh axis runs over, the one named last changes fastest.
Arguments:
- primal: float32 [2097152], P(('blk', 'grp')), may hold values from -3 to 3
- dual: float32 [1048576], P(('blk', 'grp')), may hold values from -3 to 3
- objective: float32 [2097152], P(('blk', 'grp')), may hold values from -6 to 6
- lower: float32 [2097152], P(('blk', 'grp')), may hold values from -2 to -0.5
- upper: float32 [2097152], P(('blk', 'grp')), may hold values from 0.5 to 2
- bound_kind: int32 [2097152], P(('blk', 'grp')), may hold values from 0 to 3
- rhs: float32 [1048576], P(('blk', 'grp')), may hold values from -6 to 6
- row_kind: int32 [1048576], P(('blk', 'grp')), may hold values 0 or 1
- q_tiles: float32 [4, 256, 512, 512], P('grp', 'blk'), may hold values from -0.25 to 0.25
- q_index: int32 [4, 2, 256], P('grp', None, 'blk'), may hold values from 0 to 1023
- k_tiles: float32 [4, 384, 512, 512], P('grp', 'blk'), may hold values from -0.25 to 0.25
- k_rows: int32 [4, 384], P('grp', 'blk'), may hold values from 0 to 31
- k_cols: int32 [4, 384], P('grp', 'blk'), may hold values from 0 to 1023
Outputs:
- final_primal: float32 [2097152], P(('blk', 'grp'))
- final_dual: float32 [1048576], P(('blk', 'grp'))
- primal_weight: float32 [], replicated
Inputs may be any that keep to these rules, and one draw needn't show every extreme that they name: `q_index`: row and column tile indices of Hessian tiles, within the column group. `k_rows`: row tile within the tile's dual block. `bound_kind`: 0 free, 1 lower bound only, 2 both bounds, 3 upper bound only.
All inputs are finite; a program needn't handle non-finite values. No bound on the sum of `row_kind` on one device may be relied on, other than what follows from the above.
Results may differ from a plain program's by a relative error of at most 0.00017.
Values sent between devices are 32-bit elements; how exact they have to be, the bound alone decides.
A program may use at most 64 MiB of HBM per device.

v0:
```python
import jax
import jax.numpy as jnp
from jax import lax
from jax.experimental import pallas as pl
from jax.experimental.pallas import tpu as pltpu
from jax.sharding import Mesh
from jax.sharding import PartitionSpec as P

F32 = jnp.float32
BF16 = jnp.bfloat16
MESH = pl.DeviceIdType.MESH
EPSILON = 1e-06
STEP_SCALE = 0.5
FAR = 1e30


def split3(v):
    hi = v.astype(BF16)
    rest = v - hi.astype(F32)
    mid = rest.astype(BF16)
    low = (rest - mid.astype(F32)).astype(BF16)
    return hi, mid, low


def pick(onehot, data):
    parts = [jnp.dot(onehot, part, preferred_element_type=F32) for part in split3(data)]
    return parts[0] + (parts[1] + parts[2])


def onehot(cond):
    return jnp.where(cond, 1.0, 0.0).astype(BF16)


def iota(shape, dim):
    return lax.broadcasted_iota(jnp.int32, shape, dim)


def folded(v):
    return jnp.sum(v.reshape(-1, 8, 128), axis=0)


def scalar_sum(v):
    return jnp.sum(jnp.sum(v, axis=0, keepdims=True), axis=1, keepdims=True)


def kernel(
    x_h, y_h, c_h, lo_h, hi_h, bk_h, b_h, rk_h, q_h, k_h, qi_s, kr_s, kc_s,
    xo_h, yo_h, w_s,
    tiles, bounds, kinds, rkind,
    xpl, cpl, ydat, idz, idp, idg, nidz, tid, sel, ed, ysel, e,
    sx, xr, sc, cr, xs, cst, yrows, ys, kp, zprod, sp, gp, dbuf, wz, wp,
    loc, tsem, zs, zr, ps, pr, gs, gr,
):
    z = lax.axis_index("z")
    px, py = lax.axis_index("x"), lax.axis_index("yl")
    gh, gl = lax.axis_index("yh"), lax.axis_index("co")
    p, g = px * 2 + py, gh * 2 + gl
    pending = []

    loads = {}
    for n, (name, src, dst) in enumerate((
        ("x", x_h, xpl.at[p]),
        ("y", y_h, ydat.at[g, 0]),
        ("b", b_h, ydat.at[g, 1]),
        ("rk", rk_h, rkind),
        ("c", c_h, cpl.at[p, 0]),
        ("lo", lo_h, bounds.at[0]),
        ("hi", hi_h, bounds.at[1]),
        ("bk", bk_h, kinds),
    )):
        loads[name] = pltpu.make_async_copy(src, dst, loc.at[n])
        loads[name].start()
    tile_loads = []
    for t in range(10):
        src = q_h.at[0, t] if t < 4 else k_h.at[0, t - 4]
        tile_loads.append(pltpu.make_async_copy(src, tiles.at[t], tsem.at[t]))
        tile_loads[-1].start()

    def z_peer(k):
        return {"z": lax.rem(z + k, 8)}

    def p_peer(k):
        return {"x": lax.rem(px + k // 2, 4), "yl": lax.rem(py + k % 2, 2)}

    def g_peer(k):
        return {"yh": lax.rem(gh + k // 2, 2), "co": lax.rem(gl + k % 2, 2)}

    def send(count, peer, ssem, rsem, stage, source, target):
        copies = []
        for k in range(1, count):
            copies.append(pltpu.make_async_remote_copy(
                src_ref=source(k), dst_ref=target, send_sem=ssem.at[stage, k - 1], recv_sem=rsem.at[stage, k - 1],
                device_id=peer(k), device_id_type=MESH,
            ))
            copies[-1].start()
        pending.extend(copies)
        return copies

    def send_z(stage, source, target):
        return send(8, z_peer, zs, zr, stage, source, target)

    def send_p(stage, source, target):
        return send(8, p_peer, ps, pr, stage, source, target)

    def send_g(stage, source, target):
        return send(4, g_peer, gs, gr, stage, source, target)

    def arrive(copies):
        for copy in copies:
            copy.wait_recv()

    lane, sub = iota((8, 128), 1), iota((8, 128), 0)

    def ids_at(place, ids):
        slot = place // 4
        value = jnp.zeros((8, 128), jnp.int32)
        for n, scalar in enumerate(ids):
            value = jnp.where(slot == n, scalar, value)
        return jnp.where((place >= 0) & (place < 4 * len(ids)), value * 4 + place % 4 + 1, 0)

    cons_cols = [kc_s[0, t] for t in range(6)]
    sent = [qi_s[0, 0, t] for t in range(4)] + cons_cols
    need = [qi_s[0, 1, t] for t in range(4)] + cons_cols
    rows = [kr_s[0, t] for t in range(6)]
    sent_v = ids_at(sub * 128 + lane - z * 64, sent)
    need_v = ids_at(lane, need)
    rows_v = ids_at(lane - g * 32, rows)
    ids = jnp.where(sub < 4, sent_v, jnp.where(sub == 4, need_v, jnp.where(sub == 5, rows_v, 0))).astype(F32)
    idz[z] = ids
    idp[p] = ids
    idg[g] = ids
    for zz in range(8):
        zprod[0, zz, 40:64, :] = jnp.zeros((24, 128), F32)
        zprod[1, zz, 40:64, :] = jnp.zeros((24, 128), F32)

    barrier = pltpu.get_barrier_semaphore()
    for k in range(1, 8):
        pl.semaphore_signal(barrier, inc=1, device_id=z_peer(k), device_id_type=MESH)
        pl.semaphore_signal(barrier, inc=1, device_id=p_peer(k), device_id_type=MESH)
    for k in range(1, 4):
        pl.semaphore_signal(barrier, inc=1, device_id=g_peer(k), device_id_type=MESH)
    pl.semaphore_wait(barrier, 17)

    loads["x"].wait()
    x_plane = send_p(0, lambda k: xpl.at[p], xpl.at[p])
    id_z = send_z(0, lambda k: idz.at[z], idz.at[z])
    id_p = send_p(1, lambda k: idp.at[p], idp.at[p])
    id_g = send_g(0, lambda k: idg.at[g], idg.at[g])
    loads["y"].wait()
    loads["b"].wait()
    loads["rk"].wait()
    ydat[g, 2] = rkind[...].astype(F32)
    y_all = send_g(1, lambda k: ydat.at[g], ydat.at[g])
    loads["c"].wait()
    loads["lo"].wait()
    loads["hi"].wait()
    loads["bk"].wait()
    kind = kinds[...]
    cpl[p, 1] = jnp.where((kind == 1) | (kind == 2), bounds[0], -FAR)
    cpl[p, 2] = jnp.where((kind == 2) | (kind == 3), bounds[1], FAR)
    c_plane = send_p(2, lambda k: cpl.at[p], cpl.at[p])

    arrive(id_z)
    eye40 = iota((40, 128), 0) == iota((40, 128), 1)

    def column(row, mask):
        return jnp.sum(jnp.where(mask, row, 0.0), axis=1, keepdims=True)

    for zz in range(8):
        nidz[40 * zz : 40 * zz + 40, :] = jnp.broadcast_to(column(idz[zz, 4:5, :], eye40), (40, 128))
    for n in range(4):
        have = (z * 512 + n * 128 + 1 + iota((1, 128), 1)).astype(F32)
        sel[:, n * 128 : (n + 1) * 128] = onehot(nidz[...] == have)

    arrive(x_plane)
    sx[...] = pick(sel[...], xpl[...].reshape(512, 128)).reshape(8, 40, 128)
    xr[z] = sx[z]
    x_slots = send_z(1, lambda k: sx.at[lax.rem(z + k, 8)], xr.at[z])
    xs[0, 0:64, :] = xpl[p]

    arrive(id_g)
    eye32 = iota((32, 128), 1) == iota((32, 128), 0) + g * 32
    own_rows = column(idg[g, 5:6, :], eye32)
    ysel[...] = onehot(own_rows == (iota((32, 128), 1) + 1).astype(F32))
    all_rows = idg[0, 5:6, :] + idg[1, 5:6, :] + idg[2, 5:6, :] + idg[3, 5:6, :]
    ed[...] = onehot((iota((128, 128), 0) + 1).astype(F32) == all_rows)
    arrive(id_p)
    for pp in range(8):
        own = ((z * 8 + pp) * 64 + 1 + iota((64, 128), 0)).astype(F32)
        tid[104 * pp : 104 * pp + 64, :] = own
        tid[104 * pp + 64 : 104 * pp + 104, :] = jnp.broadcast_to(column(idp[pp, 4:5, :], eye40), (40, 128))
    made = idz[0, 0:4, :]
    for zz in range(1, 8):
        made = made + idz[zz, 0:4, :]
    for n in range(4):
        e[:, n * 128 : (n + 1) * 128] = onehot(tid[...] == made[n : n + 1, :])

    eye = iota((128, 128), 0) == iota((128, 128), 1)

    def forward(first, pairs, source, store):
        def body(i, _):
            x8 = source(i)
            out = jnp.zeros((8, 128), F32)
            for h in range(2):
                for r in range(4):
                    total = None
                    for n in range(4):
                        part = tiles[first + 2 * i + h, r * 128 : (r + 1) * 128, n * 128 : (n + 1) * 128]
                        part = part * x8[4 * h + n : 4 * h + n + 1, :]
                        total = part if total is None else total + part
                    col = jnp.sum(total, axis=1, keepdims=True)
                    row = jnp.sum(jnp.where(eye, col, 0.0), axis=0, keepdims=True)
                    out = jnp.where(sub == 4 * h + r, row, out)
            store(i, out)
            return 0

        lax.fori_loop(0, pairs, body, 0)

    def transposed(stage):
        def body(i, _):
            y8 = yrows[pl.ds(pl.multiple_of(8 * i, 8), 8), :]
            out = jnp.zeros((8, 128), F32)
            for h in range(2):
                totals = [None] * 4
                for r in range(4):
                    col = column(y8[4 * h + r : 4 * h + r + 1, :], eye)
                    for n in range(4):
                        part = tiles[4 + 2 * i + h, r * 128 : (r + 1) * 128, n * 128 : (n + 1) * 128]
                        part = folded(part * col)
                        totals[n] = part if totals[n] is None else totals[n] + part
                for n in range(4):
                    row = jnp.sum(totals[n], axis=0, keepdims=True)
                    out = jnp.where(sub == 4 * h + n, row, out)
            zprod[stage, z, pl.ds(pl.multiple_of(16 + 8 * i, 8), 8), :] = -out
            return 0

        lax.fori_loop(0, 3, body, 0)

    def hess(step):
        def source(i):
            return xs[step, pl.ds(pl.multiple_of(64 + 8 * i, 8), 8), :]

        def store(i, out):
            zprod[step, z, pl.ds(pl.multiple_of(8 * i, 8), 8), :] = out

        forward(0, 2, source, store)

    def cons(step):
        def source(i):
            return xs[step, pl.ds(pl.multiple_of(80 + 8 * i, 8), 8), :]

        def store(i, out):
            kp[step, pl.ds(pl.multiple_of(8 * i, 8), 8), :] = out

        forward(4, 3, source, store)

    arrive(y_all)
    ys[0] = ydat[:, 0].reshape(128, 128)
    for copy in tile_loads:
        copy.wait()
    yrows[...] = pick(ysel[...], ys[0])
    transposed(0)

    arrive(x_slots)
    xs[0, 64:104, :] = jnp.sum(xr[...], axis=0)
    hess(0)
    prod_z = send_z(2, lambda k: zprod.at[0, z, pl.ds(0, 40)], zprod.at[0, z, pl.ds(0, 40)])

    arrive(c_plane)
    for a in range(3):
        sc[:, a] = pick(sel[...], cpl[:, a].reshape(512, 128)).reshape(8, 40, 128)
        cr[z, a] = sc[z, a]
    c_slots = send_z(3, lambda k: sc.at[lax.rem(z + k, 8)], cr.at[z])
    for a in range(3):
        cst[a, 0:64, :] = cpl[p, a]
    cons(0)

    weight = jnp.ones((1, 1), F32)
    for step in range(2):
        arrive(prod_z)
        sp[step] = pick(e[...], zprod[step].reshape(512, 128)).reshape(8, 104, 128)
        gp[step, p] = sp[step, p]
        grads = []
        for k in range(1, 8):
            to = lax.rem(px + k // 2, 4) * 2 + lax.rem(py + k % 2, 2)
            grads.append(to)
        grad_p = send_p(3 + step, lambda k: sp.at[step, grads[k - 1]], gp.at[step, p])
        if step == 0:
            arrive(c_slots)
            for a in range(3):
                cst[a, 64:104, :] = jnp.sum(cr[:, a], axis=0)
        else:
            arrive(w_p)
            sums = jnp.sum(wp[step - 1], axis=0)
            weight = jnp.sqrt(weight * jnp.sqrt((scalar_sum(sums[8:16]) + EPSILON) / (scalar_sum(sums[0:8]) + EPSILON)))
        step_primal = STEP_SCALE / weight
        step_dual = STEP_SCALE * weight
        arrive(grad_p)
        gradient = jnp.sum(gp[step], axis=0) + cst[0]
        current = xs[step]
        updated = jnp.minimum(jnp.maximum(current - step_primal * gradient, cst[1]), cst[2])
        xs[step + 1] = updated
        moved = updated[0:64] - current[0:64]
        if step == 1:
            x_out = pltpu.make_async_copy(xs.at[2, pl.ds(0, 64)], xo_h, loc.at[8])
            x_out.start()

        cons(step + 1)
        dbuf[step, g, 0:24, :] = 2.0 * kp[step + 1] - kp[step]
        dbuf[step, g, 24:32, :] = folded(moved * moved)
        duals_g = send_g(2 + step, lambda k: dbuf.at[step, g], dbuf.at[step, g])
        if step == 0:
            hess(1)
        arrive(duals_g)
        extrap = pick(ed[...], dbuf[step].reshape(128, 128))
        duals = ys[step]
        dual_new = duals + step_dual * (ydat[:, 1].reshape(128, 128) - extrap)
        dual_new = jnp.where(ydat[:, 2].reshape(128, 128) == 1.0, jnp.maximum(dual_new, 0.0), dual_new)
        ys[step + 1] = dual_new
        moved = dual_new - duals
        wz[step, z, 0:8, :] = jnp.sum(dbuf[step, :, 24:32, :], axis=0)
        wz[step, z, 8:16, :] = folded(moved * moved)
        if step == 0:
            yrows[...] = pick(ysel[...], dual_new)
            transposed(1)
            prod_z = send_z(4, lambda k: zprod.at[1, z, pl.ds(0, 40)], zprod.at[1, z, pl.ds(0, 40)])
        else:
            y_out = pltpu.make_async_copy(ys.at[2, pl.ds(pl.multiple_of(g * 32, 32), 32)], yo_h, loc.at[9])
            y_out.start()
        w_z = send_z(5 + step, lambda k: wz.at[step, z], wz.at[step, z])
        arrive(w_z)
        wp[step, p] = jnp.sum(wz[step], axis=0)
        w_p = send_p(5 + step, lambda k: wp.at[step, p], wp.at[step, p])

    arrive(w_p)
    sums = jnp.sum(wp[1], axis=0)
    weight = jnp.sqrt(weight * jnp.sqrt((scalar_sum(sums[8:16]) + EPSILON) / (scalar_sum(sums[0:8]) + EPSILON)))
    w_s[0, 0] = weight[0, 0]
    x_out.wait()
    y_out.wait()
    for copy in pending:
        copy.wait_send()


def shards(primal, dual, objective, lower, upper, bound_kind, rhs, row_kind, q_tiles, q_index, k_tiles, k_rows, k_cols):
    hbm = pl.BlockSpec(memory_space=pl.ANY)
    smem = pl.BlockSpec(memory_space=pltpu.SMEM)
    vmem, dma = pltpu.VMEM, pltpu.SemaphoreType.DMA

    def lines(v):
        return v.reshape(-1, 128)

    final_x, final_y, weight = pl.pallas_call(
        kernel,
        name="pdhg",
        out_shape=(
            jax.ShapeDtypeStruct((64, 128), F32),
            jax.ShapeDtypeStruct((32, 128), F32),
            jax.ShapeDtypeStruct((1, 1), F32),
        ),
        in_specs=[hbm] * 10 + [smem] * 3,
        out_specs=(hbm, hbm, smem),
        scratch_shapes=[
            vmem((10, 512, 512), F32),
            vmem((2, 64, 128), F32),
            vmem((64, 128), jnp.int32),
            vmem((32, 128), jnp.int32),
            vmem((8, 64, 128), F32),
            vmem((8, 3, 64, 128), F32),
            vmem((4, 3, 32, 128), F32),
            vmem((8, 8, 128), F32),
            vmem((8, 8, 128), F32),
            vmem((4, 8, 128), F32),
            vmem((320, 128), F32),
            vmem((832, 128), F32),
            vmem((320, 512), BF16),
            vmem((128, 128), BF16),
            vmem((32, 128), BF16),
            vmem((832, 512), BF16),
            vmem((8, 40, 128), F32),
            vmem((8, 40, 128), F32),
            vmem((8, 3, 40, 128), F32),
            vmem((8, 3, 40, 128), F32),
            vmem((3, 104, 128), F32),
            vmem((3, 104, 128), F32),
            vmem((32, 128), F32),
            vmem((3, 128, 128), F32),
            vmem((3, 24, 128), F32),
            vmem((2, 8, 64, 128), F32),
            vmem((2, 8, 104, 128), F32),
            vmem((2, 8, 104, 128), F32),
            vmem((2, 4, 32, 128), F32),
            vmem((2, 8, 16, 128), F32),
            vmem((2, 8, 16, 128), F32),
            dma((10,)),
            dma((10,)),
            dma((7, 7)),
            dma((7, 7)),
            dma((7, 7)),
            dma((7, 7)),
            dma((4, 3)),
            dma((4, 3)),
        ],
        compiler_params=pltpu.CompilerParams(
            collective_id=0, has_side_effects=True, vmem_limit_bytes=48 * 1024 * 1024
        ),
    )(
        lines(primal), lines(dual), lines(objective), lines(lower), lines(upper), lines(bound_kind),
        lines(rhs), lines(row_kind), q_tiles, k_tiles, q_index, k_rows, k_cols,
    )
    return final_x.reshape(-1), final_y.reshape(-1), weight.reshape(())


def solution(mesh):
    finer = Mesh(mesh.devices.reshape(2, 2, 8, 4, 2), ("yh", "co", "z", "x", "yl"))
    grp, blk, both = ("yh", "co"), ("z", "x", "yl"), ("z", "x", "yl", "yh", "co")
    placed = (P(both),) * 8 + (
        P(grp, blk, None, None),
        P(grp, None, blk),
        P(grp, blk, None, None),
        P(grp, blk),
        P(grp, blk),
    )
    return jax.shard_map(shards, mesh=finer, in_specs=placed, out_specs=(P(both), P(both), P()), check_vma=False)
```

profile of v0, /device:TPU:1, one launch (start us, length us, event | category | flops | bytes accessed | tf_op | source)
XLA Modules:
  0.0 93.8 jit_solution(14609914522184038563)
XLA Ops:
  0.6 0.0 copy-start
  0.6 2.2 %copy-done = f32[1,4,512,512]{3,2,1,0:T(8,128)S(1)} copy-done((f32[1,4,512,512]{3,2,1,0:T(8,128)S(1)}, f32[1,4,512,512]{3,2,1,0:T(8,128)}, u32[]{:S(2)}) %copy-start) | copy-done | bytes 4194328
  2.8 0.0 copy-start.1
  2.8 0.8 copy-done.1
  3.6 0.0 copy-start.2
  3.6 0.8 copy-done.2
  4.3 0.0 copy-start.3
  4.3 0.8 copy-done.3
  5.1 0.0 copy-start.4
  5.1 0.8 copy-done.4
  5.9 0.0 copy-start.5
  5.9 0.8 copy-done.5
  6.6 0.0 copy-start.6
  6.6 0.7 copy-done.6
  7.3 0.0 copy-start.7
  7.3 0.7 copy-done.7
  8.1 0.0 copy-start.8
  8.1 0.7 copy-done.8
  8.8 0.0 copy-start.9
  8.8 0.7 copy-done.9
  9.4 0.0 copy-start.10
  9.5 0.7 copy-done.10
  10.1 0.0 copy-start.11
  10.1 0.7 copy-done.11
  10.8 80.0 %pdhg.1 = (f32[64,128]{1,0:T(8,128)S(1)}, f32[32,128]{1,0:T(8,128)S(1)}, f32[1,1]{1,0:T(1,128)}) custom-call(f32[64,128]{1,0:T(8,128)S(1)} %bitcast.11, f32[32,128]{1,0:T(8,128)S(1)} %bitcast.17, f32[64,128]{1,0:T(8,128)S(1)} %bitcast.12, f32[64,128]{1,0:T(8,128)S(1)} %bitcast.13, f32[64,128]{1,0:T(8,128)S(1)} %bitcast.14, s32[64,128]{1,0:T(8,128)S(1)} %bitcast.15, ...), custom_call_target="tpu_custom_call" | custom-call | tf_op jit(solution)/shard_map/pdhg/pallas_call | solution.py:353
  90.8 0.6 copy.19
  91.4 0.6 copy.20
Async XLA Ops:
  0.6 2.2 %copy-start = (f32[1,4,512,512]{3,2,1,0:T(8,128)S(1)}, f32[1,4,512,512]{3,2,1,0:T(8,128)}, u32[]{:S(2)}) copy-start(f32[1,4,512,512]{3,2,1,0:T(8,128)} %q_h.1) | copy-start | bytes 12582916
  2.8 0.8 copy-start.1
  3.6 0.8 copy-start.2
  4.3 0.8 copy-start.3
  5.1 0.8 copy-start.4
  5.9 0.8 copy-start.5
  6.6 0.7 copy-start.6
  7.3 0.7 copy-start.7
  8.1 0.7 copy-start.8
  8.8 0.7 copy-start.9
  9.4 0.7 copy-start.10
  10.1 0.7 copy-start.11
where the time goes:
time: 94.9 us; the launch traced here: 93.8 us
  Pallas kernels  80 us (84%)
  local copies, waits for them, and re-layouts  11.3 us (12%)
  between operations  2.43 us (3%)
    pallas_call x1, Pallas kernels, shards(): pl.pallas_call(kernel, name='pdhg', out_shape=(jax.ShapeDtypeStruct((64,...  80 us
    unnamed x26, local copies, waits for them, and re-layouts  11.3 us

commit v1 on v0

v1 whole, which is shorter than its diff:
```python
import jax
import jax.numpy as jnp
from jax import lax
from jax.experimental import pallas as pl
from jax.experimental.pallas import tpu as pltpu
from jax.sharding import Mesh
from jax.sharding import PartitionSpec as P

F32 = jnp.float32
BF16 = jnp.bfloat16
MESH = pl.DeviceIdType.MESH
EPSILON = 1e-06
STEP_SCALE = 0.5
FAR = 1e30


def halves(v):
    hi = v.astype(BF16)
    mid = (v - hi.astype(F32)).astype(BF16)
    return jnp.concatenate([hi, mid], axis=1)


def pick(onehot, pair):
    both = jnp.dot(onehot, pair, preferred_element_type=F32)
    return both[:, 0:128] + both[:, 128:256]


def onehot(cond):
    return jnp.where(cond, 1.0, 0.0).astype(BF16)


def iota(shape, dim):
    return lax.broadcasted_iota(jnp.int32, shape, dim)


def folded(v):
    return jnp.sum(v.reshape(-1, 8, 128), axis=0)


def scalar_sum(v):
    return jnp.sum(jnp.sum(v, axis=0, keepdims=True), axis=1, keepdims=True)


def kernel(
    x_h, y_h, c_h, lo_h, hi_h, bk_h, b_h, rk_h, q_h, k_h, qi_h, kr_h, kc_h,
    xo_h, yo_h, w_s,
    tiles, bounds, kinds, rkind,
    xpl, cpl, y0, rows, idz, idp, idg, nid, sel, es, eo, ed, ysel,
    sx, xr, sc, cr, xs, cst, yrows, ys, kp, zprod, sps, spo, gps, gpo, dbuf, wz, wp,
    qi_s, kr_s, kc_s, loc, zs, zr, ps, pr, gs, gr, ws, wr,
):
    z = lax.axis_index("z")
    px, py = lax.axis_index("x"), lax.axis_index("yl")
    gh, gl = lax.axis_index("yh"), lax.axis_index("co")
    p, g = px * 2 + py, gh * 2 + gl
    pending = []

    def z_peer(k):
        return {"z": lax.rem(z + k, 8)}

    def p_peer(k):
        return {"x": lax.rem(px + k // 2, 4), "yl": lax.rem(py + k % 2, 2)}

    def g_peer(k):
        return {"yh": lax.rem(gh + k // 2, 2), "co": lax.rem(gl + k % 2, 2)}

    def w_peer(k):
        return {**p_peer(k // 4), **g_peer(k % 4)}

    def p_index(k):
        return lax.rem(px + k // 2, 4) * 2 + lax.rem(py + k % 2, 2)

    barrier = pltpu.get_barrier_semaphore()
    for k in range(1, 8):
        pl.semaphore_signal(barrier, inc=1, device_id=z_peer(k), device_id_type=MESH)
    for k in range(1, 32):
        pl.semaphore_signal(barrier, inc=1, device_id=w_peer(k), device_id_type=MESH)

    def load(n, *pairs):
        for src, dst in pairs:
            pltpu.make_async_copy(src, dst, loc.at[n]).start()

    def loaded(n, part):
        pltpu.make_async_copy(part, part, loc.at[n]).wait()

    index_loads = [
        pltpu.make_async_copy(src, dst, loc.at[n])
        for n, (src, dst) in enumerate(((qi_h, qi_s), (kr_h, kr_s), (kc_h, kc_s)))
    ]
    for copy in index_loads:
        copy.start()
    load(3, (x_h, xpl.at[p]))
    load(4, (y_h, y0.at[g]))
    load(5, (c_h, cpl.at[0, p]), (lo_h, bounds.at[0]), (hi_h, bounds.at[1]), (bk_h, kinds))
    load(6, (b_h, rows.at[g, 0]), (rk_h, rkind))
    load(7, *((k_h.at[0, t], tiles.at[4 + t]) for t in range(6)))
    load(8, *((q_h.at[0, t], tiles.at[t]) for t in range(4)))

    def send(count, peer, ssem, rsem, stage, source, target, whole):
        for k in range(1, count):
            pltpu.make_async_remote_copy(
                src_ref=source(k), dst_ref=target, send_sem=ssem.at[stage], recv_sem=rsem.at[stage],
                device_id=peer(k), device_id_type=MESH,
            ).start()
        pending.append((whole, ssem.at[stage]))
        return whole, rsem.at[stage]

    def send_z(stage, source, target, whole):
        return send(8, z_peer, zs, zr, stage, source, target, whole)

    def send_p(stage, source, target, whole):
        return send(8, p_peer, ps, pr, stage, source, target, whole)

    def send_g(stage, source, target, whole):
        return send(4, g_peer, gs, gr, stage, source, target, whole)

    def send_w(stage, source, target, whole):
        return send(32, w_peer, ws, wr, stage, source, target, whole)

    def arrive(stage):
        whole, sem = stage
        pltpu.make_async_copy(whole, whole, sem).wait()

    lane, sub = iota((4, 128), 1), iota((4, 128), 0)
    sub8 = iota((8, 128), 0)

    def ids_at(place, ids):
        slot = place // 4
        value = jnp.zeros((4, 128), jnp.int32)
        for n, scalar in enumerate(ids):
            value = jnp.where(slot == n, scalar, value)
        return jnp.where((place >= 0) & (place < 4 * len(ids)), value * 4 + place % 4 + 1, 0)

    for copy in index_loads:
        copy.wait()
    cons_cols = [kc_s[0, t] for t in range(6)]
    sent_v = ids_at(lane - lax.rem(z, 2) * 64, [qi_s[0, 0, t] for t in range(4)] + cons_cols)
    need_v = ids_at(lane, [qi_s[0, 1, t] for t in range(4)] + cons_cols)
    rows_v = ids_at(lane - g * 24, [kr_s[0, t] for t in range(6)])
    ids = jnp.where(sub == 0, sent_v, jnp.where(sub == 1, need_v, jnp.where(sub == 2, rows_v, 0))).astype(F32)
    idz[z] = ids
    idp[p] = ids
    idg[g] = ids
    for zz in range(8):
        zprod[0, zz, 40:64, :] = jnp.zeros((24, 128), F32)
        zprod[1, zz, 40:64, :] = jnp.zeros((24, 128), F32)

    pl.semaphore_wait(barrier, 38)

    id_z = send_z(0, lambda k: idz.at[z], idz.at[z], idz.at[pl.ds(0, 7)])
    loaded(3, x_h)
    x_plane = send_p(0, lambda k: xpl.at[p], xpl.at[p], xpl.at[pl.ds(0, 7)])
    loaded(4, y_h)
    y_all = send_g(1, lambda k: y0.at[g], y0.at[g], y0.at[pl.ds(0, 3)])
    id_g = send_g(0, lambda k: idg.at[g], idg.at[g], idg.at[pl.ds(0, 3)])
    id_p = send_p(1, lambda k: idp.at[p], idp.at[p], idp.at[pl.ds(0, 7)])
    loaded(5, cpl.at[0, pl.ds(0, 4)])
    kind = kinds[...]
    cpl[1, p] = jnp.where((kind == 1) | (kind == 2), bounds[0], -FAR)
    cpl[2, p] = jnp.where((kind == 2) | (kind == 3), bounds[1], FAR)
    c_plane = [send_p(2 + a, lambda k: cpl.at[a, p], cpl.at[a, p], cpl.at[a, pl.ds(0, 7)]) for a in range(3)]
    loaded(6, rows.at[0])
    rows[g, 1] = rkind[...].astype(F32)
    rows_all = send_g(2, lambda k: rows.at[g], rows.at[g], rows.at[pl.ds(0, 3)])

    eye40 = iota((40, 128), 0) == iota((40, 128), 1)

    def column(row, mask):
        return jnp.sum(jnp.where(mask, row, 0.0), axis=1, keepdims=True)

    arrive(id_z)
    for zz in range(8):
        nid[40 * zz : 40 * zz + 40, :] = jnp.broadcast_to(column(idz[zz, 1:2, :], eye40), (40, 128))
    for n in range(4):
        have = (z * 512 + n * 128 + 1 + iota((1, 128), 1)).astype(F32)
        sel[:, n * 128 : (n + 1) * 128] = onehot(nid[...] == have)

    arrive(x_plane)
    sx[...] = pick(sel[...], halves(xpl[...].reshape(512, 128))).reshape(8, 40, 128)
    xr[z] = sx[z]
    x_slots = send_z(1, lambda k: sx.at[lax.rem(z + k, 8)], xr.at[z], xr.at[pl.ds(0, 7)])
    xs[0, 0:64, :] = xpl[p]

    eye = iota((128, 128), 0) == iota((128, 128), 1)

    def forward(first, pairs, source, store):
        def body(i, _):
            x8 = source(i)
            out = jnp.zeros((8, 128), F32)
            for h in range(2):
                for r in range(4):
                    total = None
                    for n in range(4):
                        part = tiles[first + 2 * i + h, r * 128 : (r + 1) * 128, n * 128 : (n + 1) * 128]
                        part = part * x8[4 * h + n : 4 * h + n + 1, :]
                        total = part if total is None else total + part
                    col = jnp.sum(total, axis=1, keepdims=True)
                    row = jnp.sum(jnp.where(eye, col, 0.0), axis=0, keepdims=True)
                    out = jnp.where(sub8 == 4 * h + r, row, out)
            store(i, out)
            return 0

        lax.fori_loop(0, pairs, body, 0)

    def transposed(stage):
        def body(i, _):
            y8 = yrows[pl.ds(pl.multiple_of(8 * i, 8), 8), :]
            out = jnp.zeros((8, 128), F32)
            for h in range(2):
                totals = [None] * 4
                for r in range(4):
                    col = column(y8[4 * h + r : 4 * h + r + 1, :], eye)
                    for n in range(4):
                        part = tiles[4 + 2 * i + h, r * 128 : (r + 1) * 128, n * 128 : (n + 1) * 128]
                        part = folded(part * col)
                        totals[n] = part if totals[n] is None else totals[n] + part
                for n in range(4):
                    row = jnp.sum(totals[n], axis=0, keepdims=True)
                    out = jnp.where(sub8 == 4 * h + n, row, out)
            zprod[stage, z, pl.ds(pl.multiple_of(16 + 8 * i, 8), 8), :] = -out
            return 0

        lax.fori_loop(0, 3, body, 0)

    def hess(step):
        def source(i):
            return xs[step, pl.ds(pl.multiple_of(64 + 8 * i, 8), 8), :]

        def store(i, out):
            zprod[step, z, pl.ds(pl.multiple_of(8 * i, 8), 8), :] = out

        forward(0, 2, source, store)

    def cons(step):
        def source(i):
            return xs[step, pl.ds(pl.multiple_of(80 + 8 * i, 8), 8), :]

        def store(i, out):
            kp[step, pl.ds(pl.multiple_of(8 * i, 8), 8), :] = out

        forward(4, 3, source, store)

    def send_hess(step):
        part = zprod.at[step, z, pl.ds(0, 16)]
        return send_z(5 + 2 * step, lambda k: part, part, zprod.at[step, pl.ds(0, 7), pl.ds(0, 16)])

    def send_trans(step):
        part = zprod.at[step, z, pl.ds(16, 24)]
        return send_z(6 + 2 * step, lambda k: part, part, zprod.at[step, pl.ds(0, 7), pl.ds(16, 24)])

    arrive(id_g)
    eye32 = (iota((32, 128), 1) == iota((32, 128), 0) + g * 24) & (iota((32, 128), 0) < 24)
    ysel[...] = onehot(column(idg[g, 2:3, :], eye32) == (iota((32, 128), 1) + 1).astype(F32))
    arrive(y_all)
    ys[0] = y0[...].reshape(128, 128)
    loaded(7, tiles.at[pl.ds(0, 6)])
    yrows[...] = pick(ysel[...], halves(ys[0]))
    transposed(0)
    trans_z = send_trans(0)

    loaded(8, tiles.at[pl.ds(0, 4)])
    arrive(x_slots)
    xs[0, 64:104, :] = jnp.sum(xr[...], axis=0)
    hess(0)
    hess_z = send_hess(0)

    c_slots = []
    for a in range(3):
        arrive(c_plane[a])
        sc[a] = pick(sel[...], halves(cpl[a].reshape(512, 128))).reshape(8, 40, 128)
        cr[a, z] = sc[a, z]
        c_slots.append(
            send_z(2 + a, lambda k: sc.at[a, lax.rem(z + k, 8)], cr.at[a, z], cr.at[a, pl.ds(0, 7)])
        )
        cst[a, 0:64, :] = cpl[a, p]

    arrive(id_p)
    for pp in range(8):
        nid[40 * pp : 40 * pp + 40, :] = jnp.broadcast_to(column(idp[pp, 1:2, :], eye40), (40, 128))
    own = (z * 512 + 1 + iota((512, 128), 0)).astype(F32)
    for n in range(4):
        made = idz[2 * n, 0:1, :] + idz[2 * n + 1, 0:1, :]
        es[:, n * 128 : (n + 1) * 128] = onehot(nid[...] == made)
        eo[:, n * 128 : (n + 1) * 128] = onehot(own == made)
    all_rows = idg[0, 2:3, :] + idg[1, 2:3, :] + idg[2, 2:3, :] + idg[3, 2:3, :]
    ed[...] = onehot((iota((128, 128), 0) + 1).astype(F32) == all_rows)[:, 0:96]

    cons(0)

    def next_weight(stage, weight):
        sums = jnp.sum(wp[stage], axis=0)
        total = jnp.sum(sums, axis=1, keepdims=True) + EPSILON
        return jnp.sqrt(weight * jnp.sqrt(total[1:2] / total[0:1]))

    weight = jnp.ones((1, 1), F32)
    for step in range(2):
        arrive(trans_z)
        arrive(hess_z)
        pair = halves(zprod[step].reshape(512, 128))
        sps[step] = pick(es[...], pair).reshape(8, 40, 128)
        gps[step, p] = sps[step, p]
        first = 16 * step
        grad_s = send_p(
            5 + 2 * step,
            lambda k: sps.at[step, p_index(k), pl.ds(first, 40 - first)],
            gps.at[step, p, pl.ds(first, 40 - first)],
            gps.at[step, pl.ds(0, 7), pl.ds(first, 40 - first)],
        )
        spo[step] = pick(eo[...], pair).reshape(8, 64, 128)
        gpo[step, p] = spo[step, p]
        grad_o = send_p(6 + 2 * step, lambda k: spo.at[step, p_index(k)], gpo.at[step, p], gpo.at[step, pl.ds(0, 7)])
        if step == 0:
            for a in range(3):
                arrive(c_slots[a])
                cst[a, 64:104, :] = jnp.sum(cr[a], axis=0)
        else:
            arrive(w_p)
            weight = next_weight(0, weight)
        step_primal = STEP_SCALE / weight
        step_dual = STEP_SCALE * weight

        def advance(a, b, total):
            here = pl.ds(a, b - a)
            current = xs[step, here, :]
            moved = current - step_primal * (total + cst[0, here, :])
            updated = jnp.minimum(jnp.maximum(moved, cst[1, here, :]), cst[2, here, :])
            xs[step + 1, here, :] = updated
            return updated - current

        arrive(grad_s)
        advance(64 + first, 104, jnp.sum(gps[step, :, first:40, :], axis=0))

        cons(step + 1)
        dbuf[step, g] = 2.0 * kp[step + 1] - kp[step]
        duals_g = send_g(3 + step, lambda k: dbuf.at[step, g], dbuf.at[step, g], dbuf.at[step, pl.ds(0, 3)])
        if step == 0:
            hess(1)
            hess_z = send_hess(1)
            arrive(rows_all)
        arrive(grad_o)
        moved = advance(0, 64, jnp.sum(gpo[step], axis=0))
        wz[step, z, 0:1, :] = jnp.sum(moved * moved, axis=0, keepdims=True)
        if step == 1:
            x_out = pltpu.make_async_copy(xs.at[2, pl.ds(0, 64)], xo_h, loc.at[9])
            x_out.start()
        arrive(duals_g)
        extrap = pick(ed[...], halves(dbuf[step].reshape(96, 128)))
        duals = ys[step]
        dual_new = duals + step_dual * (rows[:, 0].reshape(128, 128) - extrap)
        dual_new = jnp.where(rows[:, 1].reshape(128, 128) == 1.0, jnp.maximum(dual_new, 0.0), dual_new)
        ys[step + 1] = dual_new
        moved = dual_new - duals
        wz[step, z, 1:2, :] = jnp.sum(moved * moved, axis=0, keepdims=True) * 0.25
        w_z = send_z(9 + step, lambda k: wz.at[step, z], wz.at[step, z], wz.at[step, pl.ds(0, 7)])
        if step == 0:
            yrows[...] = pick(ysel[...], halves(dual_new))
            transposed(1)
            trans_z = send_trans(1)
        if step == 1:
            y_out = pltpu.make_async_copy(ys.at[2, pl.ds(pl.multiple_of(g * 32, 32), 32)], yo_h, loc.at[10])
            y_out.start()
        arrive(w_z)
        wp[step, p * 4 + g] = jnp.sum(wz[step], axis=0)
        w_p = send_w(step, lambda k: wp.at[step, p * 4 + g], wp.at[step, p * 4 + g], wp.at[step, pl.ds(0, 31)])

    arrive(w_p)
    w_s[0, 0] = next_weight(1, weight)[0, 0]
    x_out.wait()
    y_out.wait()
    for stage in pending:
        arrive(stage)


def shards(primal, dual, objective, lower, upper, bound_kind, rhs, row_kind, q_tiles, q_index, k_tiles, k_rows, k_cols):
    hbm = pl.BlockSpec(memory_space=pl.ANY)
    smem = pl.BlockSpec(memory_space=pltpu.SMEM)
    vmem, dma = pltpu.VMEM, pltpu.SemaphoreType.DMA

    def lines(v):
        return v.reshape(-1, 128)

    final_x, final_y, weight = pl.pallas_call(
        kernel,
        name="pdhg",
        out_shape=(
            jax.ShapeDtypeStruct((64, 128), F32),
            jax.ShapeDtypeStruct((32, 128), F32),
            jax.ShapeDtypeStruct((1, 1), F32),
        ),
        in_specs=[hbm] * 13,
        out_specs=(hbm, hbm, smem),
        scratch_shapes=[
            vmem((10, 512, 512), F32),
            vmem((2, 64, 128), F32),
            vmem((64, 128), jnp.int32),
            vmem((32, 128), jnp.int32),
            vmem((8, 64, 128), F32),
            vmem((3, 8, 64, 128), F32),
            vmem((4, 32, 128), F32),
            vmem((4, 2, 32, 128), F32),
            vmem((8, 4, 128), F32),
            vmem((8, 4, 128), F32),
            vmem((4, 4, 128), F32),
            vmem((320, 128), F32),
            vmem((320, 512), BF16),
            vmem((320, 512), BF16),
            vmem((512, 512), BF16),
            vmem((128, 96), BF16),
            vmem((32, 128), BF16),
            vmem((8, 40, 128), F32),
            vmem((8, 40, 128), F32),
            vmem((3, 8, 40, 128), F32),
            vmem((3, 8, 40, 128), F32),
            vmem((3, 104, 128), F32),
            vmem((3, 104, 128), F32),
            vmem((32, 128), F32),
            vmem((3, 128, 128), F32),
            vmem((3, 24, 128), F32),
            vmem((2, 8, 64, 128), F32),
            vmem((2, 8, 40, 128), F32),
            vmem((2, 8, 64, 128), F32),
            vmem((2, 8, 40, 128), F32),
            vmem((2, 8, 64, 128), F32),
            vmem((2, 4, 24, 128), F32),
            vmem((2, 8, 2, 128), F32),
            vmem((2, 32, 2, 128), F32),
            pltpu.SMEM((1, 2, 4), jnp.int32),
            pltpu.SMEM((1, 6), jnp.int32),
            pltpu.SMEM((1, 6), jnp.int32),
            dma((11,)),
            dma((11,)),
            dma((11,)),
            dma((9,)),
            dma((9,)),
            dma((5,)),
            dma((5,)),
            dma((2,)),
            dma((2,)),
        ],
        compiler_params=pltpu.CompilerParams(
            collective_id=0, has_side_effects=True, vmem_limit_bytes=67043328
        ),
    )(
        lines(primal), lines(dual), lines(objective), lines(lower), lines(upper), lines(bound_kind),
        lines(rhs), lines(row_kind), q_tiles, k_tiles, q_index, k_rows, k_cols,
    )
    return final_x.reshape(-1), final_y.reshape(-1), weight.reshape(())


def solution(mesh):
    finer = Mesh(mesh.devices.reshape(2, 2, 8, 4, 2), ("yh", "co", "z", "x", "yl"))
    grp, blk, both = ("yh", "co"), ("z", "x", "yl"), ("z", "x", "yl", "yh", "co")
    placed = (P(both),) * 8 + (
        P(grp, blk, None, None),
        P(grp, None, blk),
        P(grp, blk, None, None),
        P(grp, blk),
        P(grp, blk),
    )
    return jax.shard_map(shards, mesh=finer, in_specs=placed, out_specs=(P(both), P(both), P()), check_vma=False)
```

time: 94.9 us -> 75 us (0.79)
  Pallas kernels: 80 us -> 69.7 us
  local copies, waits for them, and re-layouts: 11.3 us -> 2.7 us
    pallas_call x1, Pallas kernels: 80 us -> 69.7 us  [shards(): pl.pallas_call(kernel, name='pdhg', out_shape=(jax.ShapeDtypeStruct((64,...]
    unnamed x26 -> x2, local copies, waits for them, and re-layouts: 11.3 us -> 2.7 us
where the time goes in v1:
time: 75 us; the launch traced here: 74.8 us
  Pallas kernels  69.7 us (93%)
  local copies, waits for them, and re-layouts  2.7 us (4%)
  between operations  2.38 us (3%)
    pallas_call x1, Pallas kernels, shards(): pl.pallas_call(kernel, name='pdhg', out_shape=(jax.ShapeDtypeStruct((64,...  69.7 us
    unnamed x2, local copies, waits for them, and re-layouts  2.7 us

profile of v1, /device:TPU:1, one launch (start us, length us, event | category | flops | bytes accessed | tf_op | source)
XLA Modules:
  0.0 74.8 jit_solution(14741715836783137033)
XLA Ops:
  0.6 69.7 %pdhg.1 = (f32[64,128]{1,0:T(8,128)}, f32[32,128]{1,0:T(8,128)}, f32[1,1]{1,0:T(1,128)}) custom-call(f32[64,128]{1,0:T(8,128)} %bitcast.11, f32[32,128]{1,0:T(8,128)} %bitcast.17, f32[64,128]{1,0:T(8,128)} %bitcast.12, f32[64,128]{1,0:T(8,128)} %bitcast.13, f32[64,128]{1,0:T(8,128)} %bitcast.14, s32[64,128]{1,0:T(8,128)} %bitcast.15, f32[32,128]{1,0:T(8,128)} %bitcast.18, ...), custom_call_target="tpu_custom_call" | custom-call | tf_op jit(solution)/shard_map/pdhg/pallas_call | solution.py:382
  70.4 1.4 %copy.19 = f32[8192]{0:T(1024)} copy(f32[8192]{0:T(1024)} %bitcast.16) | data formatting | bytes 65536
  71.8 1.3 %copy.20 = f32[4096]{0:T(1024)} copy(f32[4096]{0:T(1024)} %bitcast.20) | data formatting | bytes 32768

commit v2 on v1

--- a/solution.py
+++ b/solution.py
@@ -44,7 +44,7 @@
 def kernel(
     x_h, y_h, c_h, lo_h, hi_h, bk_h, b_h, rk_h, q_h, k_h, qi_h, kr_h, kc_h,
     xo_h, yo_h, w_s,
-    tiles, bounds, kinds, rkind,
+    tiles, bounds, kinds, rkind, hz, sh, hr, nidp, selp,
     xpl, cpl, y0, rows, idz, idp, idg, nid, sel, es, eo, ed, ysel,
     sx, xr, sc, cr, xs, cst, yrows, ys, kp, zprod, sps, spo, gps, gpo, dbuf, wz, wp,
     qi_s, kr_s, kc_s, loc, zs, zr, ps, pr, gs, gr, ws, wr,
@@ -150,18 +150,20 @@
     id_z = send_z(0, lambda k: idz.at[z], idz.at[z], idz.at[pl.ds(0, 7)])
     loaded(3, x_h)
     x_plane = send_p(0, lambda k: xpl.at[p], xpl.at[p], xpl.at[pl.ds(0, 7)])
+    id_g = send_g(0, lambda k: idg.at[g], idg.at[g], idg.at[pl.ds(0, 3)])
+    id_p = send_p(1, lambda k: idp.at[p], idp.at[p], idp.at[pl.ds(0, 7)])
     loaded(4, y_h)
     y_all = send_g(1, lambda k: y0.at[g], y0.at[g], y0.at[pl.ds(0, 3)])
-    id_g = send_g(0, lambda k: idg.at[g], idg.at[g], idg.at[pl.ds(0, 3)])
-    id_p = send_p(1, lambda k: idp.at[p], idp.at[p], idp.at[pl.ds(0, 7)])
     loaded(5, cpl.at[0, pl.ds(0, 4)])
     kind = kinds[...]
     cpl[1, p] = jnp.where((kind == 1) | (kind == 2), bounds[0], -FAR)
-    cpl[2, p] = jnp.where((kind == 2) | (kind == 3), bounds[1], FAR)
-    c_plane = [send_p(2 + a, lambda k: cpl.at[a, p], cpl.at[a, p], cpl.at[a, pl.ds(0, 7)]) for a in range(3)]
+    upper = jnp.where((kind == 2) | (kind == 3), bounds[1], FAR)
+    hz[z] = upper
+    hi_line = send_z(4, lambda k: hz.at[z], hz.at[z], hz.at[pl.ds(0, 7)])
+    cst[2, 0:64, :] = upper
     loaded(6, rows.at[0])
     rows[g, 1] = rkind[...].astype(F32)
-    rows_all = send_g(2, lambda k: rows.at[g], rows.at[g], rows.at[pl.ds(0, 3)])
+    xs[0, 0:64, :] = xpl[p]
 
     eye40 = iota((40, 128), 0) == iota((40, 128), 1)
 
@@ -169,6 +171,8 @@
         return jnp.sum(jnp.where(mask, row, 0.0), axis=1, keepdims=True)
 
     arrive(id_z)
+    c_plane = [send_p(2 + a, lambda k: cpl.at[a, p], cpl.at[a, p], cpl.at[a, pl.ds(0, 7)]) for a in range(2)]
+    rows_all = send_g(2, lambda k: rows.at[g], rows.at[g], rows.at[pl.ds(0, 3)])
     for zz in range(8):
         nid[40 * zz : 40 * zz + 40, :] = jnp.broadcast_to(column(idz[zz, 1:2, :], eye40), (40, 128))
     for n in range(4):
@@ -179,7 +183,6 @@
     sx[...] = pick(sel[...], halves(xpl[...].reshape(512, 128))).reshape(8, 40, 128)
     xr[z] = sx[z]
     x_slots = send_z(1, lambda k: sx.at[lax.rem(z + k, 8)], xr.at[z], xr.at[pl.ds(0, 7)])
-    xs[0, 0:64, :] = xpl[p]
 
     eye = iota((128, 128), 0) == iota((128, 128), 1)
 
@@ -240,13 +243,23 @@
 
         forward(4, 3, source, store)
 
-    def send_hess(step):
-        part = zprod.at[step, z, pl.ds(0, 16)]
-        return send_z(5 + 2 * step, lambda k: part, part, zprod.at[step, pl.ds(0, 7), pl.ds(0, 16)])
-
-    def send_trans(step):
-        part = zprod.at[step, z, pl.ds(16, 24)]
-        return send_z(6 + 2 * step, lambda k: part, part, zprod.at[step, pl.ds(0, 7), pl.ds(16, 24)])
+    def send_products(stage, step, first, count):
+        part = zprod.at[step, z, pl.ds(first, count)]
+        return send_z(stage, lambda k: part, part, zprod.at[step, pl.ds(0, 7), pl.ds(first, count)])
+
+    def picked(a):
+        arrive(c_plane[a])
+        sc[a] = pick(sel[...], halves(cpl[a].reshape(512, 128))).reshape(8, 40, 128)
+        cr[a, z] = sc[a, z]
+        cst[a, 0:64, :] = cpl[a, p]
+
+    def send_constants(stage, a, n, first, count):
+        return send_z(
+            stage,
+            lambda k: sc.at[pl.ds(a, n), lax.rem(z + k, 8), pl.ds(first, count)],
+            cr.at[pl.ds(a, n), z, pl.ds(first, count)],
+            cr.at[pl.ds(a, n), pl.ds(0, 7), pl.ds(first, count)],
+        )
 
     arrive(id_g)
     eye32 = (iota((32, 128), 1) == iota((32, 128), 0) + g * 24) & (iota((32, 128), 0) < 24)
@@ -256,36 +269,39 @@
     loaded(7, tiles.at[pl.ds(0, 6)])
     yrows[...] = pick(ysel[...], halves(ys[0]))
     transposed(0)
-    trans_z = send_trans(0)
+    products = [send_products(10, 0, 16, 24)]
+
+    arrive(id_p)
+    for pp in range(8):
+        nidp[40 * pp : 40 * pp + 40, :] = jnp.broadcast_to(column(idp[pp, 1:2, :], eye40), (40, 128))
+    for n in range(4):
+        at = n * 128 + iota((1, 128), 1)
+        have = (((at // 64) * 8 + p) * 64 + at % 64 + 1).astype(F32)
+        selp[:, n * 128 : (n + 1) * 128] = onehot(nidp[...] == have)
+    arrive(hi_line)
+    sh[...] = pick(selp[...], halves(hz[...].reshape(512, 128))).reshape(8, 40, 128)
+    hr[p] = sh[p]
+    hi_slots = send_p(9, lambda k: sh.at[p_index(k)], hr.at[p], hr.at[pl.ds(0, 7)])
 
     loaded(8, tiles.at[pl.ds(0, 4)])
     arrive(x_slots)
     xs[0, 64:104, :] = jnp.sum(xr[...], axis=0)
     hess(0)
-    hess_z = send_hess(0)
-
-    c_slots = []
-    for a in range(3):
-        arrive(c_plane[a])
-        sc[a] = pick(sel[...], halves(cpl[a].reshape(512, 128))).reshape(8, 40, 128)
-        cr[a, z] = sc[a, z]
-        c_slots.append(
-            send_z(2 + a, lambda k: sc.at[a, lax.rem(z + k, 8)], cr.at[a, z], cr.at[a, pl.ds(0, 7)])
-        )
-        cst[a, 0:64, :] = cpl[a, p]
-
-    arrive(id_p)
-    for pp in range(8):
-        nid[40 * pp : 40 * pp + 40, :] = jnp.broadcast_to(column(idp[pp, 1:2, :], eye40), (40, 128))
+    products.append(send_products(5, 0, 0, 16))
+
+    picked(0)
+    picked(1)
+
     own = (z * 512 + 1 + iota((512, 128), 0)).astype(F32)
     for n in range(4):
         made = idz[2 * n, 0:1, :] + idz[2 * n + 1, 0:1, :]
-        es[:, n * 128 : (n + 1) * 128] = onehot(nid[...] == made)
+        es[:, n * 128 : (n + 1) * 128] = onehot(nidp[...] == made)
         eo[:, n * 128 : (n + 1) * 128] = onehot(own == made)
     all_rows = idg[0, 2:3, :] + idg[1, 2:3, :] + idg[2, 2:3, :] + idg[3, 2:3, :]
     ed[...] = onehot((iota((128, 128), 0) + 1).astype(F32) == all_rows)[:, 0:96]
 
     cons(0)
+    cons_all = send_constants(2, 0, 2, 16, 24)
 
     def next_weight(stage, weight):
         sums = jnp.sum(wp[stage], axis=0)
@@ -294,8 +310,8 @@
 
     weight = jnp.ones((1, 1), F32)
     for step in range(2):
-        arrive(trans_z)
-        arrive(hess_z)
+        for stage in products:
+            arrive(stage)
         pair = halves(zprod[step].reshape(512, 128))
         sps[step] = pick(es[...], pair).reshape(8, 40, 128)
         gps[step, p] = sps[step, p]
@@ -308,12 +324,15 @@
         )
         spo[step] = pick(eo[...], pair).reshape(8, 64, 128)
         gpo[step, p] = spo[step, p]
+        if step == 0:
+            hess_all = send_constants(3, 0, 2, 0, 16)
+            arrive(hi_slots)
+            cst[2, 64:104, :] = jnp.sum(hr[...], axis=0)
+            arrive(cons_all)
+            for a in range(2):
+                cst[a, 80:104, :] = jnp.sum(cr[a, :, 16:40, :], axis=0)
         grad_o = send_p(6 + 2 * step, lambda k: spo.at[step, p_index(k)], gpo.at[step, p], gpo.at[step, pl.ds(0, 7)])
-        if step == 0:
-            for a in range(3):
-                arrive(c_slots[a])
-                cst[a, 64:104, :] = jnp.sum(cr[a], axis=0)
-        else:
+        if step == 1:
             arrive(w_p)
             weight = next_weight(0, weight)
         step_primal = STEP_SCALE / weight
@@ -328,14 +347,18 @@
             return updated - current
 
         arrive(grad_s)
-        advance(64 + first, 104, jnp.sum(gps[step, :, first:40, :], axis=0))
+        advance(80, 104, jnp.sum(gps[step, :, 16:40, :], axis=0))
 
         cons(step + 1)
         dbuf[step, g] = 2.0 * kp[step + 1] - kp[step]
         duals_g = send_g(3 + step, lambda k: dbuf.at[step, g], dbuf.at[step, g], dbuf.at[step, pl.ds(0, 3)])
         if step == 0:
+            arrive(hess_all)
+            for a in range(2):
+                cst[a, 64:80, :] = jnp.sum(cr[a, :, 0:16, :], axis=0)
+            advance(64, 80, jnp.sum(gps[0, :, 0:16, :], axis=0))
             hess(1)
-            hess_z = send_hess(1)
+            products = [send_products(6, 1, 0, 16)]
             arrive(rows_all)
         arrive(grad_o)
         moved = advance(0, 64, jnp.sum(gpo[step], axis=0))
@@ -351,11 +374,11 @@
         ys[step + 1] = dual_new
         moved = dual_new - duals
         wz[step, z, 1:2, :] = jnp.sum(moved * moved, axis=0, keepdims=True) * 0.25
-        w_z = send_z(9 + step, lambda k: wz.at[step, z], wz.at[step, z], wz.at[step, pl.ds(0, 7)])
+        w_z = send_z(8 + step, lambda k: wz.at[step, z], wz.at[step, z], wz.at[step, pl.ds(0, 7)])
         if step == 0:
             yrows[...] = pick(ysel[...], halves(dual_new))
             transposed(1)
-            trans_z = send_trans(1)
+            products.append(send_products(7, 1, 16, 24))
         if step == 1:
             y_out = pltpu.make_async_copy(ys.at[2, pl.ds(pl.multiple_of(g * 32, 32), 32)], yo_h, loc.at[10])
             y_out.start()
@@ -373,6 +396,7 @@
 
 def shards(primal, dual, objective, lower, upper, bound_kind, rhs, row_kind, q_tiles, q_index, k_tiles, k_rows, k_cols):
     hbm = pl.BlockSpec(memory_space=pl.ANY)
+    anywhere = pl.BlockSpec(memory_space=pl.ANY)
     smem = pl.BlockSpec(memory_space=pltpu.SMEM)
     vmem, dma = pltpu.VMEM, pltpu.SemaphoreType.DMA
 
@@ -388,14 +412,19 @@
             jax.ShapeDtypeStruct((1, 1), F32),
         ),
         in_specs=[hbm] * 13,
-        out_specs=(hbm, hbm, smem),
+        out_specs=(anywhere, anywhere, smem),
         scratch_shapes=[
             vmem((10, 512, 512), F32),
             vmem((2, 64, 128), F32),
             vmem((64, 128), jnp.int32),
             vmem((32, 128), jnp.int32),
             vmem((8, 64, 128), F32),
-            vmem((3, 8, 64, 128), F32),
+            vmem((8, 40, 128), F32),
+            vmem((8, 40, 128), F32),
+            vmem((320, 128), F32),
+            vmem((320, 512), BF16),
+            vmem((8, 64, 128), F32),
+            vmem((2, 8, 64, 128), F32),
             vmem((4, 32, 128), F32),
             vmem((4, 2, 32, 128), F32),
             vmem((8, 4, 128), F32),
@@ -409,8 +438,8 @@
             vmem((32, 128), BF16),
             vmem((8, 40, 128), F32),
             vmem((8, 40, 128), F32),
-            vmem((3, 8, 40, 128), F32),
-            vmem((3, 8, 40, 128), F32),
+            vmem((2, 8, 40, 128), F32),
+            vmem((2, 8, 40, 128), F32),
             vmem((3, 104, 128), F32),
             vmem((3, 104, 128), F32),
             vmem((32, 128), F32),
@@ -430,8 +459,8 @@
             dma((11,)),
             dma((11,)),
             dma((11,)),
-            dma((9,)),
-            dma((9,)),
+            dma((10,)),
+            dma((10,)),
             dma((5,)),
             dma((5,)),
             dma((2,)),

time: 75 us -> 72.4 us (0.965)
  Pallas kernels: 69.7 us -> 67.1 us
    pallas_call x1, Pallas kernels: 69.7 us -> 67.1 us  [shards(): pl.pallas_call(kernel, name='pdhg', out_shape=(jax.ShapeDtypeStruct((64,...]
where the time goes in v2:
time: 72.4 us; the launch traced here: 72.2 us
  Pallas kernels  67.1 us (93%)
  local copies, waits for them, and re-layouts  2.7 us (4%)
  between operations  2.38 us (3%)
    pallas_call x1, Pallas kernels, shards(): pl.pallas_call(kernel, name='pdhg', out_shape=(jax.ShapeDtypeStruct((64,...  67.1 us
    unnamed x2, local copies, waits for them, and re-layouts  2.7 us

profile of v2, /device:TPU:1, one launch (start us, length us, event | category | flops | bytes accessed | tf_op | source)
XLA Modules:
  0.0 72.2 jit_solution(2304227121711056369)
XLA Ops:
  0.6 67.1 %pdhg.1 = (f32[64,128]{1,0:T(8,128)}, f32[32,128]{1,0:T(8,128)}, f32[1,1]{1,0:T(1,128)}) custom-call(f32[64,128]{1,0:T(8,128)} %bitcast.11, f32[32,128]{1,0:T(8,128)} %bitcast.17, f32[64,128]{1,0:T(8,128)} %bitcast.12, f32[64,128]{1,0:T(8,128)} %bitcast.13, f32[64,128]{1,0:T(8,128)} %bitcast.14, s32[64,128]{1,0:T(8,128)} %bitcast.15, f32[32,128]{1,0:T(8,128)} %bitcast.18, ...), custom_call_target="tpu_custom_call" | custom-call | tf_op jit(solution)/shard_map/pdhg/pallas_call | solution.py:406
  67.8 1.4 %copy.19 = f32[8192]{0:T(1024)} copy(f32[8192]{0:T(1024)} %bitcast.16) | data formatting | bytes 65536
  69.1 1.3 %copy.20 = f32[4096]{0:T(1024)} copy(f32[4096]{0:T(1024)} %bitcast.20) | data formatting | bytes 32768

commit v3 on v2

--- a/solution.py
+++ b/solution.py
@@ -43,11 +43,11 @@
 
 def kernel(
     x_h, y_h, c_h, lo_h, hi_h, bk_h, b_h, rk_h, q_h, k_h, qi_h, kr_h, kc_h,
-    xo_h, yo_h, w_s,
+    xo, yo, w_s,
     tiles, bounds, kinds, rkind, hz, sh, hr, nidp, selp,
     xpl, cpl, y0, rows, idz, idp, idg, nid, sel, es, eo, ed, ysel,
-    sx, xr, sc, cr, xs, cst, yrows, ys, kp, zprod, sps, spo, gps, gpo, dbuf, wz, wp,
-    qi_s, kr_s, kc_s, loc, zs, zr, ps, pr, gs, gr, ws, wr,
+    sx, xr, sc, cr, xs, cst, yrows, ys, kp, zprod, sps, spo, gps, gpo, dbuf, wz, wp, wg,
+    qi_s, kr_s, kc_s, loc, zs, zr, ps, pr, gs, gr,
 ):
     z = lax.axis_index("z")
     px, py = lax.axis_index("x"), lax.axis_index("yl")
@@ -64,17 +64,15 @@
     def g_peer(k):
         return {"yh": lax.rem(gh + k // 2, 2), "co": lax.rem(gl + k % 2, 2)}
 
-    def w_peer(k):
-        return {**p_peer(k // 4), **g_peer(k % 4)}
-
     def p_index(k):
         return lax.rem(px + k // 2, 4) * 2 + lax.rem(py + k % 2, 2)
 
     barrier = pltpu.get_barrier_semaphore()
     for k in range(1, 8):
         pl.semaphore_signal(barrier, inc=1, device_id=z_peer(k), device_id_type=MESH)
-    for k in range(1, 32):
-        pl.semaphore_signal(barrier, inc=1, device_id=w_peer(k), device_id_type=MESH)
+        pl.semaphore_signal(barrier, inc=1, device_id=p_peer(k), device_id_type=MESH)
+    for k in range(1, 4):
+        pl.semaphore_signal(barrier, inc=1, device_id=g_peer(k), device_id_type=MESH)
 
     def load(n, *pairs):
         for src, dst in pairs:
@@ -113,9 +111,6 @@
 
     def send_g(stage, source, target, whole):
         return send(4, g_peer, gs, gr, stage, source, target, whole)
-
-    def send_w(stage, source, target, whole):
-        return send(32, w_peer, ws, wr, stage, source, target, whole)
 
     def arrive(stage):
         whole, sem = stage
@@ -145,7 +140,7 @@
         zprod[0, zz, 40:64, :] = jnp.zeros((24, 128), F32)
         zprod[1, zz, 40:64, :] = jnp.zeros((24, 128), F32)
 
-    pl.semaphore_wait(barrier, 38)
+    pl.semaphore_wait(barrier, 17)
 
     id_z = send_z(0, lambda k: idz.at[z], idz.at[z], idz.at[pl.ds(0, 7)])
     loaded(3, x_h)
@@ -182,7 +177,16 @@
     arrive(x_plane)
     sx[...] = pick(sel[...], halves(xpl[...].reshape(512, 128))).reshape(8, 40, 128)
     xr[z] = sx[z]
-    x_slots = send_z(1, lambda k: sx.at[lax.rem(z + k, 8)], xr.at[z], xr.at[pl.ds(0, 7)])
+
+    def send_x(stage, first, count):
+        return send_z(
+            stage,
+            lambda k: sx.at[lax.rem(z + k, 8), pl.ds(first, count)],
+            xr.at[z, pl.ds(first, count)],
+            xr.at[pl.ds(0, 7), pl.ds(first, count)],
+        )
+
+    x_hess = send_x(1, 0, 16)
 
     eye = iota((128, 128), 0) == iota((128, 128), 1)
 
@@ -203,7 +207,7 @@
             store(i, out)
             return 0
 
-        lax.fori_loop(0, pairs, body, 0)
+        lax.fori_loop(0, pairs, body, 0, unroll=True)
 
     def transposed(stage):
         def body(i, _):
@@ -223,7 +227,7 @@
             zprod[stage, z, pl.ds(pl.multiple_of(16 + 8 * i, 8), 8), :] = -out
             return 0
 
-        lax.fori_loop(0, 3, body, 0)
+        lax.fori_loop(0, 3, body, 0, unroll=True)
 
     def hess(step):
         def source(i):
@@ -270,6 +274,7 @@
     yrows[...] = pick(ysel[...], halves(ys[0]))
     transposed(0)
     products = [send_products(10, 0, 16, 24)]
+    x_cons = send_x(11, 16, 24)
 
     arrive(id_p)
     for pp in range(8):
@@ -284,8 +289,8 @@
     hi_slots = send_p(9, lambda k: sh.at[p_index(k)], hr.at[p], hr.at[pl.ds(0, 7)])
 
     loaded(8, tiles.at[pl.ds(0, 4)])
-    arrive(x_slots)
-    xs[0, 64:104, :] = jnp.sum(xr[...], axis=0)
+    arrive(x_hess)
+    xs[0, 64:80, :] = jnp.sum(xr[:, 0:16, :], axis=0)
     hess(0)
     products.append(send_products(5, 0, 0, 16))
 
@@ -300,41 +305,53 @@
     all_rows = idg[0, 2:3, :] + idg[1, 2:3, :] + idg[2, 2:3, :] + idg[3, 2:3, :]
     ed[...] = onehot((iota((128, 128), 0) + 1).astype(F32) == all_rows)[:, 0:96]
 
-    cons(0)
-    cons_all = send_constants(2, 0, 2, 16, 24)
-
-    def next_weight(stage, weight):
-        sums = jnp.sum(wp[stage], axis=0)
+
+    def next_weight(sums, weight):
         total = jnp.sum(sums, axis=1, keepdims=True) + EPSILON
         return jnp.sqrt(weight * jnp.sqrt(total[1:2] / total[0:1]))
 
     weight = jnp.ones((1, 1), F32)
     for step in range(2):
-        for stage in products:
-            arrive(stage)
+        arrive(products[0])
+        if step == 0:
+            cons_all = send_constants(2, 0, 2, 16, 24)
+        arrive(products[1])
         pair = halves(zprod[step].reshape(512, 128))
         sps[step] = pick(es[...], pair).reshape(8, 40, 128)
         gps[step, p] = sps[step, p]
-        first = 16 * step
-        grad_s = send_p(
-            5 + 2 * step,
-            lambda k: sps.at[step, p_index(k), pl.ds(first, 40 - first)],
-            gps.at[step, p, pl.ds(first, 40 - first)],
-            gps.at[step, pl.ds(0, 7), pl.ds(first, 40 - first)],
-        )
+
+        def send_slots(stage, first, count):
+            return send_p(
+                stage,
+                lambda k: sps.at[step, p_index(k), pl.ds(first, count)],
+                gps.at[step, p, pl.ds(first, count)],
+                gps.at[step, pl.ds(0, 7), pl.ds(first, count)],
+            )
+
+        def send_own():
+            return send_p(6 + 2 * step, lambda k: spo.at[step, p_index(k)], gpo.at[step, p], gpo.at[step, pl.ds(0, 7)])
+
+        grad_s = send_slots(5 + 2 * step, 16, 24)
+        if step == 0:
+            grad_h = send_slots(10, 0, 16)
         spo[step] = pick(eo[...], pair).reshape(8, 64, 128)
         gpo[step, p] = spo[step, p]
         if step == 0:
+            arrive(x_cons)
+            xs[0, 80:104, :] = jnp.sum(xr[:, 16:40, :], axis=0)
+            cons(0)
+            grad_o = send_own()
             hess_all = send_constants(3, 0, 2, 0, 16)
             arrive(hi_slots)
             cst[2, 64:104, :] = jnp.sum(hr[...], axis=0)
             arrive(cons_all)
             for a in range(2):
                 cst[a, 80:104, :] = jnp.sum(cr[a, :, 16:40, :], axis=0)
-        grad_o = send_p(6 + 2 * step, lambda k: spo.at[step, p_index(k)], gpo.at[step, p], gpo.at[step, pl.ds(0, 7)])
+        if step == 1:
+            grad_o = send_own()
         if step == 1:
             arrive(w_p)
-            weight = next_weight(0, weight)
+            weight = next_weight(jnp.sum(wp[0], axis=0), weight)
         step_primal = STEP_SCALE / weight
         step_dual = STEP_SCALE * weight
 
@@ -354,6 +371,7 @@
         duals_g = send_g(3 + step, lambda k: dbuf.at[step, g], dbuf.at[step, g], dbuf.at[step, pl.ds(0, 3)])
         if step == 0:
             arrive(hess_all)
+            arrive(grad_h)
             for a in range(2):
                 cst[a, 64:80, :] = jnp.sum(cr[a, :, 0:16, :], axis=0)
             advance(64, 80, jnp.sum(gps[0, :, 0:16, :], axis=0))
@@ -362,41 +380,39 @@
             arrive(rows_all)
         arrive(grad_o)
         moved = advance(0, 64, jnp.sum(gpo[step], axis=0))
-        wz[step, z, 0:1, :] = jnp.sum(moved * moved, axis=0, keepdims=True)
+        wg[step, g] = jnp.sum(moved * moved, axis=0, keepdims=True)
+        w_g = send_g(5 + step, lambda k: wg.at[step, g], wg.at[step, g], wg.at[step, pl.ds(0, 3)])
         if step == 1:
-            x_out = pltpu.make_async_copy(xs.at[2, pl.ds(0, 64)], xo_h, loc.at[9])
-            x_out.start()
+            xo[...] = xs[2, 0:64, :]
         arrive(duals_g)
         extrap = pick(ed[...], halves(dbuf[step].reshape(96, 128)))
         duals = ys[step]
         dual_new = duals + step_dual * (rows[:, 0].reshape(128, 128) - extrap)
         dual_new = jnp.where(rows[:, 1].reshape(128, 128) == 1.0, jnp.maximum(dual_new, 0.0), dual_new)
         ys[step + 1] = dual_new
-        moved = dual_new - duals
-        wz[step, z, 1:2, :] = jnp.sum(moved * moved, axis=0, keepdims=True) * 0.25
-        w_z = send_z(8 + step, lambda k: wz.at[step, z], wz.at[step, z], wz.at[step, pl.ds(0, 7)])
         if step == 0:
             yrows[...] = pick(ysel[...], halves(dual_new))
             transposed(1)
             products.append(send_products(7, 1, 16, 24))
-        if step == 1:
-            y_out = pltpu.make_async_copy(ys.at[2, pl.ds(pl.multiple_of(g * 32, 32), 32)], yo_h, loc.at[10])
-            y_out.start()
+        else:
+            yo[...] = ys[2, pl.ds(pl.multiple_of(g * 32, 32), 32), :]
+        moved = dual_new - duals
+        wz[step, z, 1:2, :] = jnp.sum(moved * moved, axis=0, keepdims=True)
+        arrive(w_g)
+        wz[step, z, 0:1, :] = jnp.sum(wg[step], axis=0)
+        w_z = send_z(8 + step, lambda k: wz.at[step, z], wz.at[step, z], wz.at[step, pl.ds(0, 7)])
         arrive(w_z)
-        wp[step, p * 4 + g] = jnp.sum(wz[step], axis=0)
-        w_p = send_w(step, lambda k: wp.at[step, p * 4 + g], wp.at[step, p * 4 + g], wp.at[step, pl.ds(0, 31)])
+        wp[step, p] = jnp.sum(wz[step], axis=0)
+        w_p = send_p((4, 11)[step], lambda k: wp.at[step, p], wp.at[step, p], wp.at[step, pl.ds(0, 7)])
 
     arrive(w_p)
-    w_s[0, 0] = next_weight(1, weight)[0, 0]
-    x_out.wait()
-    y_out.wait()
+    w_s[0, 0] = next_weight(jnp.sum(wp[1], axis=0), weight)[0, 0]
     for stage in pending:
         arrive(stage)
 
 
 def shards(primal, dual, objective, lower, upper, bound_kind, rhs, row_kind, q_tiles, q_index, k_tiles, k_rows, k_cols):
     hbm = pl.BlockSpec(memory_space=pl.ANY)
-    anywhere = pl.BlockSpec(memory_space=pl.ANY)
     smem = pl.BlockSpec(memory_space=pltpu.SMEM)
     vmem, dma = pltpu.VMEM, pltpu.SemaphoreType.DMA
 
@@ -407,12 +423,12 @@
         kernel,
         name="pdhg",
         out_shape=(
-            jax.ShapeDtypeStruct((64, 128), F32),
-            jax.ShapeDtypeStruct((32, 128), F32),
+            vmem((64, 128), F32),
+            vmem((32, 128), F32),
             jax.ShapeDtypeStruct((1, 1), F32),
         ),
         in_specs=[hbm] * 13,
-        out_specs=(anywhere, anywhere, smem),
+        out_specs=(pl.BlockSpec(memory_space=vmem), pl.BlockSpec(memory_space=vmem), smem),
         scratch_shapes=[
             vmem((10, 512, 512), F32),
             vmem((2, 64, 128), F32),
@@ -452,22 +468,21 @@
             vmem((2, 8, 64, 128), F32),
             vmem((2, 4, 24, 128), F32),
             vmem((2, 8, 2, 128), F32),
-            vmem((2, 32, 2, 128), F32),
+            vmem((2, 8, 2, 128), F32),
+            vmem((2, 4, 1, 128), F32),
             pltpu.SMEM((1, 2, 4), jnp.int32),
             pltpu.SMEM((1, 6), jnp.int32),
             pltpu.SMEM((1, 6), jnp.int32),
-            dma((11,)),
-            dma((11,)),
-            dma((11,)),
-            dma((10,)),
-            dma((10,)),
-            dma((5,)),
-            dma((5,)),
-            dma((2,)),
-            dma((2,)),
+            dma((9,)),
+            dma((12,)),
+            dma((12,)),
+            dma((12,)),
+            dma((12,)),
+            dma((7,)),
+            dma((7,)),
         ],
         compiler_params=pltpu.CompilerParams(
-            collective_id=0, has_side_effects=True, vmem_limit_bytes=67043328
+            collective_id=0, has_side_effects=True, vmem_limit_bytes=67043328 - 128 * 1024
         ),
     )(
         lines(primal), lines(dual), lines(objective), lines(lower), lines(upper), lines(bound_kind),

time: 72.4 us -> 66.5 us (0.919)
  Pallas kernels: 67.1 us -> 62.3 us
  local copies, waits for them, and re-layouts: 2.7 us -> 1.22 us
    pallas_call x1, Pallas kernels: 67.1 us -> 62.3 us  [shards(): pl.pallas_call(kernel, name='pdhg', out_shape=(vmem((64, 128), F32), vmem...]
    unnamed x2, local copies, waits for them, and re-layouts: 2.7 us -> 1.22 us
where the time goes in v3:
time: 66.5 us; the launch traced here: 65.9 us
  Pallas kernels  62.3 us (94%)
  between operations  2.33 us (4%)
  local copies, waits for them, and re-layouts  1.22 us (2%)
    pallas_call x1, Pallas kernels, shards(): pl.pallas_call(kernel, name='pdhg', out_shape=(vmem((64, 128), F32), vmem...  62.3 us

profile of v3, /device:TPU:1, one launch (start us, length us, event | category | flops | bytes accessed | tf_op | source)
XLA Modules:
  0.0 65.9 jit_solution(7787842293175066444)
XLA Ops:
  0.6 62.3 %pdhg.1 = (f32[64,128]{1,0:T(8,128)S(1)}, f32[32,128]{1,0:T(8,128)S(1)}, f32[1,1]{1,0:T(1,128)}) custom-call(f32[64,128]{1,0:T(8,128)} %bitcast.13, f32[32,128]{1,0:T(8,128)} %bitcast.18, f32[64,128]{1,0:T(8,128)} %bitcast.14, f32[64,128]{1,0:T(8,128)} %bitcast.15, f32[64,128]{1,0:T(8,128)} %bitcast.16, s32[64,128]{1,0:T(8,128)} %bitcast.17, ...), custom_call_target="tpu_custom_call" | custom-call | tf_op jit(solution)/shard_map/pdhg/pallas_call | solution.py:422
  63.0 0.6 copy.19
  63.6 0.6 copy.20

commit v4 on v3

--- a/solution.py
+++ b/solution.py
@@ -12,6 +12,9 @@
 EPSILON = 1e-06
 STEP_SCALE = 0.5
 FAR = 1e30
+Z_ORDER = (4, 3, 5, 2, 6, 1, 7)
+P_ORDER = (5, 4, 3, 7, 2, 6, 1)
+G_ORDER = (3, 2, 1)
 
 
 def halves(v):
@@ -68,10 +71,11 @@
         return lax.rem(px + k // 2, 4) * 2 + lax.rem(py + k % 2, 2)
 
     barrier = pltpu.get_barrier_semaphore()
-    for k in range(1, 8):
+    for k in Z_ORDER:
         pl.semaphore_signal(barrier, inc=1, device_id=z_peer(k), device_id_type=MESH)
+    for k in P_ORDER:
         pl.semaphore_signal(barrier, inc=1, device_id=p_peer(k), device_id_type=MESH)
-    for k in range(1, 4):
+    for k in G_ORDER:
         pl.semaphore_signal(barrier, inc=1, device_id=g_peer(k), device_id_type=MESH)
 
     def load(n, *pairs):
@@ -94,8 +98,8 @@
     load(7, *((k_h.at[0, t], tiles.at[4 + t]) for t in range(6)))
     load(8, *((q_h.at[0, t], tiles.at[t]) for t in range(4)))
 
-    def send(count, peer, ssem, rsem, stage, source, target, whole):
-        for k in range(1, count):
+    def send(order, peer, ssem, rsem, stage, source, target, whole):
+        for k in order:
             pltpu.make_async_remote_copy(
                 src_ref=source(k), dst_ref=target, send_sem=ssem.at[stage], recv_sem=rsem.at[stage],
                 device_id=peer(k), device_id_type=MESH,
@@ -104,13 +108,13 @@
         return whole, rsem.at[stage]
 
     def send_z(stage, source, target, whole):
-        return send(8, z_peer, zs, zr, stage, source, target, whole)
+        return send(Z_ORDER, z_peer, zs, zr, stage, source, target, whole)
 
     def send_p(stage, source, target, whole):
-        return send(8, p_peer, ps, pr, stage, source, target, whole)
+        return send(P_ORDER, p_peer, ps, pr, stage, source, target, whole)
 
     def send_g(stage, source, target, whole):
-        return send(4, g_peer, gs, gr, stage, source, target, whole)
+        return send(G_ORDER, g_peer, gs, gr, stage, source, target, whole)
 
     def arrive(stage):
         whole, sem = stage
@@ -166,8 +170,6 @@
         return jnp.sum(jnp.where(mask, row, 0.0), axis=1, keepdims=True)
 
     arrive(id_z)
-    c_plane = [send_p(2 + a, lambda k: cpl.at[a, p], cpl.at[a, p], cpl.at[a, pl.ds(0, 7)]) for a in range(2)]
-    rows_all = send_g(2, lambda k: rows.at[g], rows.at[g], rows.at[pl.ds(0, 3)])
     for zz in range(8):
         nid[40 * zz : 40 * zz + 40, :] = jnp.broadcast_to(column(idz[zz, 1:2, :], eye40), (40, 128))
     for n in range(4):
@@ -187,6 +189,8 @@
         )
 
     x_hess = send_x(1, 0, 16)
+    c_plane = [send_p(2 + a, lambda k: cpl.at[a, p], cpl.at[a, p], cpl.at[a, pl.ds(0, 7)]) for a in range(2)]
+    rows_all = send_g(2, lambda k: rows.at[g], rows.at[g], rows.at[pl.ds(0, 3)])
 
     eye = iota((128, 128), 0) == iota((128, 128), 1)
 
@@ -332,14 +336,13 @@
             return send_p(6 + 2 * step, lambda k: spo.at[step, p_index(k)], gpo.at[step, p], gpo.at[step, pl.ds(0, 7)])
 
         grad_s = send_slots(5 + 2 * step, 16, 24)
-        if step == 0:
-            grad_h = send_slots(10, 0, 16)
         spo[step] = pick(eo[...], pair).reshape(8, 64, 128)
         gpo[step, p] = spo[step, p]
         if step == 0:
             arrive(x_cons)
             xs[0, 80:104, :] = jnp.sum(xr[:, 16:40, :], axis=0)
             cons(0)
+            grad_h = send_slots(10, 0, 16)
             grad_o = send_own()
             hess_all = send_constants(3, 0, 2, 0, 16)
             arrive(hi_slots)

time: 66.5 us -> 63 us (0.947)
  Pallas kernels: 62.3 us -> 58.6 us
    pallas_call x1, Pallas kernels: 62.3 us -> 58.6 us  [shards(): pl.pallas_call(kernel, name='pdhg', out_shape=(vmem((64, 128), F32), vmem...]
where the time goes in v4:
time: 63 us; the launch traced here: 62.1 us
  Pallas kernels  58.6 us (93%)
  between operations  2.33 us (4%)
  local copies, waits for them, and re-layouts  1.22 us (2%)
    pallas_call x1, Pallas kernels, shards(): pl.pallas_call(kernel, name='pdhg', out_shape=(vmem((64, 128), F32), vmem...  58.6 us

profile of v4, /device:TPU:1, one launch (start us, length us, event | category | flops | bytes accessed | tf_op | source)
XLA Modules:
  0.0 62.1 jit_solution(15528270787168282118)
XLA Ops:
  0.6 58.6 %pdhg.1 = (f32[64,128]{1,0:T(8,128)S(1)}, f32[32,128]{1,0:T(8,128)S(1)}, f32[1,1]{1,0:T(1,128)}) custom-call(f32[64,128]{1,0:T(8,128)} %bitcast.13, f32[32,128]{1,0:T(8,128)} %bitcast.18, f32[64,128]{1,0:T(8,128)} %bitcast.14, f32[64,128]{1,0:T(8,128)} %bitcast.15, f32[64,128]{1,0:T(8,128)} %bitcast.16, s32[64,128]{1,0:T(8,128)} %bitcast.17, ...), custom_call_target="tpu_custom_call" | custom-call | tf_op jit(solution)/shard_map/pdhg/pallas_call | solution.py:425
  59.2 0.6 copy.19
  59.8 0.6 copy.20

commit v5 on v4

--- a/solution.py
+++ b/solution.py
@@ -1,3 +1,5 @@
+import math
+
 import jax
 import jax.numpy as jnp
 from jax import lax
@@ -14,6 +16,7 @@
 FAR = 1e30
 Z_ORDER = (4, 3, 5, 2, 6, 1, 7)
 P_ORDER = (5, 4, 3, 7, 2, 6, 1)
+OWN_ORDER = (5, 3, 7, 1, 4, 2, 6)
 G_ORDER = (3, 2, 1)
 
 
@@ -48,15 +51,15 @@
     x_h, y_h, c_h, lo_h, hi_h, bk_h, b_h, rk_h, q_h, k_h, qi_h, kr_h, kc_h,
     xo, yo, w_s,
     tiles, bounds, kinds, rkind, hz, sh, hr, nidp, selp,
-    xpl, cpl, y0, rows, idz, idp, idg, nid, sel, es, eo, ed, ysel,
-    sx, xr, sc, cr, xs, cst, yrows, ys, kp, zprod, sps, spo, gps, gpo, dbuf, wz, wp, wg,
-    qi_s, kr_s, kc_s, loc, zs, zr, ps, pr, gs, gr,
+    xpl, cpl, y0, rows, idz, idp, idg, nid, selq, selk, esk, esq, eo, ed, ysel,
+    sx, xr, sc, cr, xs, cst, yrows, ys, kp, zprod, spk, spq, spo, gpk, gpq, gpo, dbuf, wz, wp, wg,
+    qi_s, kr_s, kc_s, lines, loc, ssems, zr, pr, gr,
 ):
     z = lax.axis_index("z")
     px, py = lax.axis_index("x"), lax.axis_index("yl")
     gh, gl = lax.axis_index("yh"), lax.axis_index("co")
     p, g = px * 2 + py, gh * 2 + gl
-    pending = []
+    sent = [0, 0, 0]
 
     def z_peer(k):
         return {"z": lax.rem(z + k, 8)}
@@ -98,23 +101,24 @@
     load(7, *((k_h.at[0, t], tiles.at[4 + t]) for t in range(6)))
     load(8, *((q_h.at[0, t], tiles.at[t]) for t in range(4)))
 
-    def send(order, peer, ssem, rsem, stage, source, target, whole):
+    def send(axis, order, peer, rsem, stage, source, target, whole):
+        ssem = ssems.at[axis]
         for k in order:
             pltpu.make_async_remote_copy(
-                src_ref=source(k), dst_ref=target, send_sem=ssem.at[stage], recv_sem=rsem.at[stage],
+                src_ref=source(k), dst_ref=target, send_sem=ssem, recv_sem=rsem.at[stage],
                 device_id=peer(k), device_id_type=MESH,
             ).start()
-        pending.append((whole, ssem.at[stage]))
+        sent[axis] += 4 * math.prod(whole.shape)
         return whole, rsem.at[stage]
 
     def send_z(stage, source, target, whole):
-        return send(Z_ORDER, z_peer, zs, zr, stage, source, target, whole)
-
-    def send_p(stage, source, target, whole):
-        return send(P_ORDER, p_peer, ps, pr, stage, source, target, whole)
+        return send(0, Z_ORDER, z_peer, zr, stage, source, target, whole)
+
+    def send_p(stage, source, target, whole, order=P_ORDER):
+        return send(1, order, p_peer, pr, stage, source, target, whole)
 
     def send_g(stage, source, target, whole):
-        return send(G_ORDER, g_peer, gs, gr, stage, source, target, whole)
+        return send(2, G_ORDER, g_peer, gr, stage, source, target, whole)
 
     def arrive(stage):
         whole, sem = stage
@@ -172,13 +176,15 @@
     arrive(id_z)
     for zz in range(8):
         nid[40 * zz : 40 * zz + 40, :] = jnp.broadcast_to(column(idz[zz, 1:2, :], eye40), (40, 128))
+    wanted = nid[...].reshape(8, 40, 128)
     for n in range(4):
         have = (z * 512 + n * 128 + 1 + iota((1, 128), 1)).astype(F32)
-        sel[:, n * 128 : (n + 1) * 128] = onehot(nid[...] == have)
+        selq[:, n * 128 : (n + 1) * 128] = onehot(wanted[:, 0:16].reshape(128, 128) == have)
+        selk[:, n * 128 : (n + 1) * 128] = onehot(wanted[:, 16:40].reshape(192, 128) == have)
 
     arrive(x_plane)
-    sx[...] = pick(sel[...], halves(xpl[...].reshape(512, 128))).reshape(8, 40, 128)
-    xr[z] = sx[z]
+    pair = halves(xpl[...].reshape(512, 128))
+    sx[:, 0:16] = pick(selq[...], pair).reshape(8, 16, 128)
 
     def send_x(stage, first, count):
         return send_z(
@@ -189,6 +195,8 @@
         )
 
     x_hess = send_x(1, 0, 16)
+    sx[:, 16:40] = pick(selk[...], pair).reshape(8, 24, 128)
+    xr[z] = sx[z]
     c_plane = [send_p(2 + a, lambda k: cpl.at[a, p], cpl.at[a, p], cpl.at[a, pl.ds(0, 7)]) for a in range(2)]
     rows_all = send_g(2, lambda k: rows.at[g], rows.at[g], rows.at[pl.ds(0, 3)])
 
@@ -257,7 +265,9 @@
 
     def picked(a):
         arrive(c_plane[a])
-        sc[a] = pick(sel[...], halves(cpl[a].reshape(512, 128))).reshape(8, 40, 128)
+        pair = halves(cpl[a].reshape(512, 128))
+        sc[a, :, 0:16] = pick(selq[...], pair).reshape(8, 16, 128)
+        sc[a, :, 16:40] = pick(selk[...], pair).reshape(8, 24, 128)
         cr[a, z] = sc[a, z]
         cst[a, 0:64, :] = cpl[a, p]
 
@@ -302,9 +312,11 @@
     picked(1)
 
     own = (z * 512 + 1 + iota((512, 128), 0)).astype(F32)
+    slots = nidp[...].reshape(8, 40, 128)
     for n in range(4):
         made = idz[2 * n, 0:1, :] + idz[2 * n + 1, 0:1, :]
-        es[:, n * 128 : (n + 1) * 128] = onehot(nidp[...] == made)
+        esk[:, n * 128 : (n + 1) * 128] = onehot(slots[:, 16:40].reshape(192, 128) == made)
+        esq[:, n * 128 : (n + 1) * 128] = onehot(slots[:, 0:16].reshape(128, 128) == made)
         eo[:, n * 128 : (n + 1) * 128] = onehot(own == made)
     all_rows = idg[0, 2:3, :] + idg[1, 2:3, :] + idg[2, 2:3, :] + idg[3, 2:3, :]
     ed[...] = onehot((iota((128, 128), 0) + 1).astype(F32) == all_rows)[:, 0:96]
@@ -313,6 +325,11 @@
     def next_weight(sums, weight):
         total = jnp.sum(sums, axis=1, keepdims=True) + EPSILON
         return jnp.sqrt(weight * jnp.sqrt(total[1:2] / total[0:1]))
+
+    def sum_over_plane(step, w_z):
+        arrive(w_z)
+        wp[step, p] = jnp.sum(wz[step], axis=0)
+        return send_p((4, 11)[step], lambda k: wp.at[step, p], wp.at[step, p], wp.at[step, pl.ds(0, 7)])
 
     weight = jnp.ones((1, 1), F32)
     for step in range(2):
@@ -321,28 +338,26 @@
             cons_all = send_constants(2, 0, 2, 16, 24)
         arrive(products[1])
         pair = halves(zprod[step].reshape(512, 128))
-        sps[step] = pick(es[...], pair).reshape(8, 40, 128)
-        gps[step, p] = sps[step, p]
-
-        def send_slots(stage, first, count):
-            return send_p(
-                stage,
-                lambda k: sps.at[step, p_index(k), pl.ds(first, count)],
-                gps.at[step, p, pl.ds(first, count)],
-                gps.at[step, pl.ds(0, 7), pl.ds(first, count)],
-            )
+        spk[step] = pick(esk[...], pair).reshape(8, 24, 128)
+        gpk[step, p] = spk[step, p]
+        grad_s = send_p(
+            5 + 2 * step, lambda k: spk.at[step, p_index(k)], gpk.at[step, p], gpk.at[step, pl.ds(0, 7)]
+        )
 
         def send_own():
-            return send_p(6 + 2 * step, lambda k: spo.at[step, p_index(k)], gpo.at[step, p], gpo.at[step, pl.ds(0, 7)])
-
-        grad_s = send_slots(5 + 2 * step, 16, 24)
+            return send_p(6 + 2 * step, lambda k: spo.at[step, p_index(k)], gpo.at[step, p], gpo.at[step, pl.ds(0, 7)], OWN_ORDER)
+
+        if step == 1:
+            w_p = sum_over_plane(0, w_z)
         spo[step] = pick(eo[...], pair).reshape(8, 64, 128)
         gpo[step, p] = spo[step, p]
         if step == 0:
             arrive(x_cons)
             xs[0, 80:104, :] = jnp.sum(xr[:, 16:40, :], axis=0)
             cons(0)
-            grad_h = send_slots(10, 0, 16)
+            spq[...] = pick(esq[...], pair).reshape(8, 16, 128)
+            gpq[p] = spq[p]
+            grad_h = send_p(10, lambda k: spq.at[p_index(k)], gpq.at[p], gpq.at[pl.ds(0, 7)])
             grad_o = send_own()
             hess_all = send_constants(3, 0, 2, 0, 16)
             arrive(hi_slots)
@@ -367,26 +382,26 @@
             return updated - current
 
         arrive(grad_s)
-        advance(80, 104, jnp.sum(gps[step, :, 16:40, :], axis=0))
+        advance(80, 104, jnp.sum(gpk[step], axis=0))
 
         cons(step + 1)
         dbuf[step, g] = 2.0 * kp[step + 1] - kp[step]
         duals_g = send_g(3 + step, lambda k: dbuf.at[step, g], dbuf.at[step, g], dbuf.at[step, pl.ds(0, 3)])
-        if step == 0:
-            arrive(hess_all)
-            arrive(grad_h)
-            for a in range(2):
-                cst[a, 64:80, :] = jnp.sum(cr[a, :, 0:16, :], axis=0)
-            advance(64, 80, jnp.sum(gps[0, :, 0:16, :], axis=0))
-            hess(1)
-            products = [send_products(6, 1, 0, 16)]
-            arrive(rows_all)
         arrive(grad_o)
         moved = advance(0, 64, jnp.sum(gpo[step], axis=0))
         wg[step, g] = jnp.sum(moved * moved, axis=0, keepdims=True)
         w_g = send_g(5 + step, lambda k: wg.at[step, g], wg.at[step, g], wg.at[step, pl.ds(0, 3)])
         if step == 1:
             xo[...] = xs[2, 0:64, :]
+        if step == 0:
+            arrive(hess_all)
+            arrive(grad_h)
+            for a in range(2):
+                cst[a, 64:80, :] = jnp.sum(cr[a, :, 0:16, :], axis=0)
+            advance(64, 80, jnp.sum(gpq[...], axis=0))
+            hess(1)
+            products = [send_products(6, 1, 0, 16)]
+            arrive(rows_all)
         arrive(duals_g)
         extrap = pick(ed[...], halves(dbuf[step].reshape(96, 128)))
         duals = ys[step]
@@ -404,14 +419,13 @@
         arrive(w_g)
         wz[step, z, 0:1, :] = jnp.sum(wg[step], axis=0)
         w_z = send_z(8 + step, lambda k: wz.at[step, z], wz.at[step, z], wz.at[step, pl.ds(0, 7)])
-        arrive(w_z)
-        wp[step, p] = jnp.sum(wz[step], axis=0)
-        w_p = send_p((4, 11)[step], lambda k: wp.at[step, p], wp.at[step, p], wp.at[step, pl.ds(0, 7)])
+        if step == 1:
+            w_p = sum_over_plane(1, w_z)
 
     arrive(w_p)
     w_s[0, 0] = next_weight(jnp.sum(wp[1], axis=0), weight)[0, 0]
-    for stage in pending:
-        arrive(stage)
+    for axis in range(3):
+        arrive((lines.at[pl.ds(0, sent[axis] // 1024)], ssems.at[axis]))
 
 
 def shards(primal, dual, objective, lower, upper, bound_kind, rhs, row_kind, q_tiles, q_index, k_tiles, k_rows, k_cols):
@@ -450,8 +464,10 @@
             vmem((8, 4, 128), F32),
             vmem((4, 4, 128), F32),
             vmem((320, 128), F32),
-            vmem((320, 512), BF16),
-            vmem((320, 512), BF16),
+            vmem((128, 512), BF16),
+            vmem((192, 512), BF16),
+            vmem((192, 512), BF16),
+            vmem((128, 512), BF16),
             vmem((512, 512), BF16),
             vmem((128, 96), BF16),
             vmem((32, 128), BF16),
@@ -465,9 +481,11 @@
             vmem((3, 128, 128), F32),
             vmem((3, 24, 128), F32),
             vmem((2, 8, 64, 128), F32),
-            vmem((2, 8, 40, 128), F32),
+            vmem((2, 8, 24, 128), F32),
+            vmem((8, 16, 128), F32),
             vmem((2, 8, 64, 128), F32),
-            vmem((2, 8, 40, 128), F32),
+            vmem((2, 8, 24, 128), F32),
+            vmem((8, 16, 128), F32),
             vmem((2, 8, 64, 128), F32),
             vmem((2, 4, 24, 128), F32),
             vmem((2, 8, 2, 128), F32),
@@ -476,12 +494,11 @@
             pltpu.SMEM((1, 2, 4), jnp.int32),
             pltpu.SMEM((1, 6), jnp.int32),
             pltpu.SMEM((1, 6), jnp.int32),
+            vmem((1600, 2, 128), F32),
             dma((9,)),
+            dma((3,)),
+            dma((16,)),
             dma((12,)),
-            dma((12,)),
-            dma((12,)),
-            dma((12,)),
-            dma((7,)),
             dma((7,)),
         ],
         compiler_params=pltpu.CompilerParams(

time: 63 us -> 62.7 us (level)
  no operation moved by 1% of the time
where the time goes in v5:
time: 62.7 us; the launch traced here: 61.9 us
  Pallas kernels  58.4 us (93%)
  between operations  2.33 us (4%)
  local copies, waits for them, and re-layouts  1.22 us (2%)
    pallas_call x1, Pallas kernels, shards(): pl.pallas_call(kernel, name='pdhg', out_shape=(vmem((64, 128), F32), vmem...  58.4 us

profile of v5, /device:TPU:1, one launch (start us, length us, event | category | flops | bytes accessed | tf_op | source)
XLA Modules:
  0.0 61.9 jit_solution(1379354496925982962)
XLA Ops:
  0.6 58.4 %pdhg.1 = (f32[64,128]{1,0:T(8,128)S(1)}, f32[32,128]{1,0:T(8,128)S(1)}, f32[1,1]{1,0:T(1,128)}) custom-call(f32[64,128]{1,0:T(8,128)} %bitcast.13, f32[32,128]{1,0:T(8,128)} %bitcast.18, f32[64,128]{1,0:T(8,128)} %bitcast.14, f32[64,128]{1,0:T(8,128)} %bitcast.15, f32[64,128]{1,0:T(8,128)} %bitcast.16, s32[64,128]{1,0:T(8,128)} %bitcast.17, ...), custom_call_target="tpu_custom_call" | custom-call | tf_op jit(solution)/shard_map/pdhg/pallas_call | solution.py:439
  59.0 0.6 copy.19
  59.6 0.6 copy.20

commit v6 on v5

--- a/solution.py
+++ b/solution.py
@@ -426,6 +426,14 @@
     w_s[0, 0] = next_weight(jnp.sum(wp[1], axis=0), weight)[0, 0]
     for axis in range(3):
         arrive((lines.at[pl.ds(0, sent[axis] // 1024)], ssems.at[axis]))
+
+
+def deliver(x, y, xo, yo, sem):
+    copies = [pltpu.make_async_copy(x, xo, sem.at[0]), pltpu.make_async_copy(y, yo, sem.at[1])]
+    for copy in copies:
+        copy.start()
+    for copy in copies:
+        copy.wait()
 
 
 def shards(primal, dual, objective, lower, upper, bound_kind, rhs, row_kind, q_tiles, q_index, k_tiles, k_rows, k_cols):
@@ -508,6 +516,15 @@
         lines(primal), lines(dual), lines(objective), lines(lower), lines(upper), lines(bound_kind),
         lines(rhs), lines(row_kind), q_tiles, k_tiles, q_index, k_rows, k_cols,
     )
+    final_x, final_y = pl.pallas_call(
+        deliver,
+        name="deliver",
+        out_shape=(jax.ShapeDtypeStruct((64, 128), F32), jax.ShapeDtypeStruct((32, 128), F32)),
+        in_specs=[pl.BlockSpec(memory_space=vmem)] * 2,
+        out_specs=(hbm, hbm),
+        scratch_shapes=[dma((2,))],
+        compiler_params=pltpu.CompilerParams(vmem_limit_bytes=1024 * 1024),
+    )(final_x, final_y)
     return final_x.reshape(-1), final_y.reshape(-1), weight.reshape(())
 
 

time: 62.7 us -> 62.2 us (level)
  local copies, waits for them, and re-layouts: 1.22 us -> 0 us
    unnamed x2 -> x0, local copies, waits for them, and re-layouts: 1.22 us -> none
    pallas_call x0 -> x1, Pallas kernels: none -> 0.64 us  [shards(): pl.pallas_call(deliver, name='deliver', out_shape=(jax.ShapeDtypeStruct((...]
where the time goes in v6:
time: 62.2 us; the launch traced here: 61.4 us
  Pallas kernels  59 us (95%)
  between operations  2.41 us (4%)
    pallas_call x1, Pallas kernels, shards(): pl.pallas_call(kernel, name='pdhg', out_shape=(vmem((64, 128), F32), vmem...  58.4 us

profile of v6, /device:TPU:1, one launch (start us, length us, event | category | flops | bytes accessed | tf_op | source)
XLA Modules:
  0.0 61.4 jit_solution(18098179543564116879)
XLA Ops:
  0.6 58.4 %pdhg.1 = (f32[64,128]{1,0:T(8,128)S(1)}, f32[32,128]{1,0:T(8,128)S(1)}, f32[1,1]{1,0:T(1,128)}) custom-call(f32[64,128]{1,0:T(8,128)} %bitcast.11, f32[32,128]{1,0:T(8,128)} %bitcast.16, f32[64,128]{1,0:T(8,128)} %bitcast.12, f32[64,128]{1,0:T(8,128)} %bitcast.13, f32[64,128]{1,0:T(8,128)} %bitcast.14, s32[64,128]{1,0:T(8,128)} %bitcast.15, ...), custom_call_target="tpu_custom_call" | custom-call | tf_op jit(solution)/shard_map/pdhg/pallas_call | solution.py:447
  59.0 0.6 %deliver.1 = (f32[64,128]{1,0:T(8,128)}, f32[32,128]{1,0:T(8,128)}) custom-call(f32[64,128]{1,0:T(8,128)S(1)} %get-tuple-element.8.x, f32[32,128]{1,0:T(8,128)S(1)} %get-tuple-element.9.y), custom_call_target="tpu_custom_call" | custom-call | tf_op jit(solution)/shard_map/deliver/pallas_call | solution.py:519

commit v7 on v6

--- a/solution.py
+++ b/solution.py
@@ -150,9 +150,9 @@
 
     pl.semaphore_wait(barrier, 17)
 
-    id_z = send_z(0, lambda k: idz.at[z], idz.at[z], idz.at[pl.ds(0, 7)])
     loaded(3, x_h)
     x_plane = send_p(0, lambda k: xpl.at[p], xpl.at[p], xpl.at[pl.ds(0, 7)])
+    id_z = send_z(0, lambda k: idz.at[z], idz.at[z], idz.at[pl.ds(0, 7)])
     id_g = send_g(0, lambda k: idg.at[g], idg.at[g], idg.at[pl.ds(0, 3)])
     id_p = send_p(1, lambda k: idp.at[p], idp.at[p], idp.at[pl.ds(0, 7)])
     loaded(4, y_h)
@@ -505,7 +505,7 @@
             vmem((1600, 2, 128), F32),
             dma((9,)),
             dma((3,)),
-            dma((16,)),
+            dma((12,)),
             dma((12,)),
             dma((7,)),
         ],

time: 62.2 us -> 62.2 us (level)
  no operation moved by 1% of the time
where the time goes in v7:
time: 62.2 us; the launch traced here: 61.4 us
  Pallas kernels  59 us (95%)
  between operations  2.41 us (4%)
    pallas_call x1, Pallas kernels, shards(): pl.pallas_call(kernel, name='pdhg', out_shape=(vmem((64, 128), F32), vmem...  58.3 us

profile of v7, /device:TPU:1, one launch (start us, length us, event | category | flops | bytes accessed | tf_op | source)
XLA Modules:
  0.0 61.4 jit_solution(3353278617896400265)
XLA Ops:
  0.6 58.3 %pdhg.1 = (f32[64,128]{1,0:T(8,128)S(1)}, f32[32,128]{1,0:T(8,128)S(1)}, f32[1,1]{1,0:T(1,128)}) custom-call(f32[64,128]{1,0:T(8,128)} %bitcast.11, f32[32,128]{1,0:T(8,128)} %bitcast.16, f32[64,128]{1,0:T(8,128)} %bitcast.12, f32[64,128]{1,0:T(8,128)} %bitcast.13, f32[64,128]{1,0:T(8,128)} %bitcast.14, s32[64,128]{1,0:T(8,128)} %bitcast.15, ...), custom_call_target="tpu_custom_call" | custom-call | tf_op jit(solution)/shard_map/pdhg/pallas_call | solution.py:447
  59.0 0.6 %deliver.1 = (f32[64,128]{1,0:T(8,128)}, f32[32,128]{1,0:T(8,128)}) custom-call(f32[64,128]{1,0:T(8,128)S(1)} %get-tuple-element.8.x, f32[32,128]{1,0:T(8,128)S(1)} %get-tuple-element.9.y), custom_call_target="tpu_custom_call" | custom-call | tf_op jit(solution)/shard_map/deliver/pallas_call | solution.py:519
